TPU v7x, 128 devices: a whole 4x4x4 slice. The times are simulated.
128 devices in a mesh: dp: 1, tp: 16 (over z, y), pp: 8 (over x, core).
Axes of the slice: x: 4, y: 4, z: 4, core: 2. Of those that a mesh axis runs over, the one named last changes fastest.
Arguments:
- tokens: int32 [32, 64], P('dp')
- labels: int32 [32, 64], P('dp')
- emb_table: bfloat16 [50304, 1024], P('tp')
- w_in: bfloat16 [8, 1024, 4096], P('pp', None, 'tp')
- w_out: bfloat16 [8, 4096, 1024], P('pp', 'tp')
Outputs:
- output 1: float32 [1], P('dp')
- output 2: float32 [8, 1024, 4096], P(('dp', 'pp'), None, 'tp')
- output 3: float32 [8, 4096, 1024], P(('dp', 'pp'), 'tp')
- output 4: float32 [50304, 1024], P(('dp', 'tp'))
All inputs are finite; a program needn't handle non-finite values.
Results may differ from a plain program's by a relative error of at most 0.012808.
Values are sent between devices in bfloat16 or wider.
A program may use at most 1 GiB of HBM per device.

v0:
```python
import functools

import jax
import jax.numpy as jnp
from jax import lax
from jax.experimental import pallas as pl
from jax.experimental.pallas import tpu as pltpu
from jax.sharding import PartitionSpec as P

NORM_EPS = 1e-6
SIDE = 4
MESH = pl.DeviceIdType.MESH
F32 = jnp.float32
BF16 = jnp.bfloat16
CUBE = 0.044715
ROOT = 0.7978845608028654


def contract(lhs, rhs, lhs_dim, rhs_dim):
    return lax.dot_general(lhs, rhs, (((lhs_dim,), (rhs_dim,)), ((), ())), preferred_element_type=F32)


def gelu(h):
    return h * (0.5 * (1.0 + jnp.tanh(ROOT * (h + CUBE * (h * h * h)))))


def gelu_slope(h):
    sq = h * h
    t = jnp.tanh(ROOT * (h + CUBE * (sq * h)))
    return 0.5 * (1.0 + t) + (0.5 * h) * (1.0 - t * t) * (ROOT * (1.0 + (3.0 * CUBE) * sq))


def remote(src, dst, send, recv, where):
    return pltpu.make_async_remote_copy(src_ref=src, dst_ref=dst, send_sem=send, recv_sem=recv, device_id=where, device_id_type=MESH)


def signal(peer):
    pl.semaphore_signal(pltpu.get_barrier_semaphore(), inc=1, device_id=peer, device_id_type=MESH)


class Plane:
    def __init__(self):
        self.tp = lax.axis_index('tp')
        self.y = lax.rem(self.tp, SIDE)
        self.z = self.tp // SIDE

    def at(self, dy, dz):
        return lax.rem(self.z + dz + SIDE, SIDE) * SIDE + lax.rem(self.y + dy + SIDE, SIDE)

    def blk(self, half, df, ds):
        return self.at(df, ds) if half == 0 else self.at(ds, df)

    def near(self):
        return [{'tp': self.at(1, 0)}, {'tp': self.at(-1, 0)}, {'tp': self.at(0, 1)}, {'tp': self.at(0, -1)}]

    def rings(self):
        return [{'tp': self.at(d, 0)} for d in (1, 2, 3)] + [{'tp': self.at(0, d)} for d in (1, 2, 3)]


HOPS = (0, -1, 1, 2)
WALK = ((0, -1, None, 1), (0, 1, None, -1), (-1, 2, 0, 1), (1, 2, 1, -1))
BOTH = (0, 1)
TILE = 256
SLOTS = 15


def plane_gather(plane, bufs, send_sem, recv_sem, on_block=lambda *_: None, base=0, begun=False):
    def msg(a, half, slot, block, part, to):
        buf, start, size = bufs[a]
        size = size // 2
        start = start + half * size
        if part is not None:
            size = size // 2
            start = start + part * size
        ref = buf.at[plane.blk(half, *block), pl.ds(start, size)]
        return remote(ref, ref, send_sem.at[base + a], recv_sem.at[((base + a) * 2 + half) * SLOTS + slot], {'tp': plane.blk(half, *to)})

    def f(a, half, k, end):
        step = WALK[k]
        return msg(a, half, min(k, 2), (step[end], 0), None if end and k > 1 else step[2], (step[3], 0))

    def s(a, half, j, k, end):
        step = WALK[k]
        return msg(a, half, 3 * (j + 1) + min(k, 2), (HOPS[j], step[end]), None if end and k > 1 else step[2], (0, step[3]))

    send, recv = BOTH
    pairs = [(a, half) for a in range(len(bufs)) for half in BOTH]

    def across(a, half, j):
        for k in BOTH:
            s(a, half, j, k, send).start()
        on_block(a, half, j, 0)

    def onward(a, half, j):
        for k in BOTH:
            s(a, half, j, k, recv).wait_recv()
            s(a, half, j, k + 2, send).start()
            on_block(a, half, j, k + 1)

    if not begun:
        for pair in pairs:
            for k in BOTH:
                f(*pair, k, send).start()
            across(*pair, 0)
        yield
    for pair in pairs:
        for k in BOTH:
            f(*pair, k, recv).wait_recv()
            f(*pair, k + 2, send).start()
            across(*pair, k + 1)
    yield
    for pair in pairs:
        onward(*pair, 0)
    yield
    for pair in pairs:
        f(*pair, 2, recv).wait_recv()
        across(*pair, SIDE - 1)
    yield
    for j in range(1, SIDE):
        for pair in pairs:
            onward(*pair, j)
        yield
    for j in range(SIDE):
        for pair in pairs:
            s(*pair, j, 2, recv).wait_recv()
            on_block(*pair, j, SIDE - 1)
    for a, (buf, start, size) in enumerate(bufs):
        sent = buf.at[pl.ds(0, SIDE * SIDE - 1), pl.ds(start, size)]
        remote(sent, sent, send_sem.at[base + a], recv_sem.at[0], {'tp': plane.at(1, 0)}).wait_send()


def tiles(width):
    return [slice(n, n + TILE) for n in range(0, width, TILE)]


def drain(steps):
    for _ in steps:
        pass


def local(src, dst, sem):
    return pltpu.make_async_copy(src, dst, sem)


class Reduce:
    def __init__(self, plane, parts, got_one, sum_one, got_two, one_send, one_recv, two_send, two_recv):
        self.plane, self.parts, self.got_one, self.sum_one, self.got_two = plane, parts, got_one, sum_one, got_two
        self.one_send, self.one_recv, self.two_send, self.two_recv = one_send, one_recv, two_send, two_recv

    def row(self, half, index):
        size = self.parts.shape[3] // 2
        cols = pl.ds(half * size, size)
        return self.parts.at[:, index, :, cols] if half == 0 else self.parts.at[index, :, :, cols]

    def here(self, half):
        return (self.plane.y, self.plane.z) if half == 0 else (self.plane.z, self.plane.y)

    def first(self, half, d):
        n = half * 3 + d - 1
        dest = lax.rem(self.here(half)[0] + d, SIDE)
        return remote(self.row(half, dest), self.got_one.at[n], self.one_send, self.one_recv.at[half], {'tp': self.plane.blk(half, d, 0)})

    def second(self, half, d):
        n = half * 3 + d - 1
        dest = lax.rem(self.here(half)[1] + d, SIDE)
        return remote(self.sum_one.at[half, dest], self.got_two.at[n], self.two_send, self.two_recv.at[half], {'tp': self.plane.blk(half, 0, d)})

    def whole(self, got, send, recv, half=None):
        ref = got if half is None else got.at[pl.ds(half * 3, 3)]
        return remote(ref, ref, send, recv.at[half or 0], {'tp': self.plane.at(1, 0)})

    def begin(self, half):
        for d in (2, 1, 3):
            self.first(half, d).start()

    def middle(self):
        for half in BOTH:
            total = self.row(half, self.here(half)[0])[:].astype(F32)
            self.whole(self.got_one, self.one_send, self.one_recv, half).wait_recv()
            for d in (1, 3, 2):
                total = total + self.got_one[half * 3 + d - 1].astype(F32)
            self.sum_one[half] = total.astype(self.sum_one.dtype)
            for d in (2, 1, 3):
                self.second(half, d).start()

    def end(self):
        sums = []
        for half in BOTH:
            total = self.sum_one[half, self.here(half)[1]].astype(F32)
            self.whole(self.got_two, self.two_send, self.two_recv, half).wait_recv()
            for d in (1, 3, 2):
                total = total + self.got_two[half * 3 + d - 1].astype(F32)
            sums.append(total)
        return sums

    def close(self):
        self.whole(self.got_one, self.one_send, self.one_recv).wait_send()
        self.whole(self.got_two, self.two_send, self.two_recv).wait_send()


def fold(op, value):
    rows, cols = value.shape
    return op(value.reshape(rows // 8, 8, cols), axis=0)


def flatten(ids, flat):
    size, cols = ids.shape[1], flat.shape[1]
    for r in range(ids.shape[0]):
        at = r * size
        flat[at // cols:at // cols + 1, at % cols:at % cols + size] = ids[r:r + 1, :]


def list_rows(tokens, base, rows, group, unit, flat, slot, out):
    lines, lanes = flat.shape
    count = lines * lanes
    flatten(tokens, flat)
    row = flat[:] - base
    mine = (row >= 0) & (row < rows)
    upper = lax.broadcasted_iota(jnp.int32, (lanes, lanes), 0) <= lax.broadcasted_iota(jnp.int32, (lanes, lanes), 1)
    ones = [jnp.where(mask, 1.0, 0.0).astype(BF16) for mask in (mine, upper)]
    seen = jnp.dot(*ones, preferred_element_type=F32)
    total = jnp.zeros((1, 1), F32)
    for r in range(lines):
        line = slice(r, r + 1)
        here = slice(r * lanes, (r + 1) * lanes)
        slot[:1, here] = jnp.where(mine[line], seen[line] + (total - 1.0), -1.0).astype(jnp.int32)
        slot[1:, here] = row[line]
        total = total + seen[line, lanes - 1:]
    number = lax.broadcasted_iota(jnp.int32, (1, count), 1)
    inner = lax.rem(number, group)
    place = inner // unit * (count // group * unit) + number // group * unit + lax.rem(number, unit)
    digits = [part for value in (place, slot[1:, :]) for part in (value // 256, lax.rem(value, 256))]
    which = lax.broadcasted_iota(jnp.int32, (16, count), 0)
    values = sum(jnp.where(which == i, digit, 0) for i, digit in enumerate(digits)).astype(F32).astype(BF16)

    @pl.loop(0, count // group)
    def _(c):
        start = pl.multiple_of(c * group, group)
        pick = jnp.where(slot[:1, :] == start + lax.broadcasted_iota(jnp.int32, (group, count), 0), 1.0, 0.0).astype(BF16)
        found = contract(values, pick, 1, 1)
        for i in BOTH:
            out[i:i + 1, pl.ds(start, group)] = (found[2 * i:2 * i + 1] * 256.0 + found[2 * i + 1:2 * i + 2]).astype(jnp.int32)

    out[2:, :] = jnp.broadcast_to(total, (1, count)).astype(jnp.int32)


def forward_kernel(last, tokens, emb, w_one, w_two, y_out, order_out, hid_out, one_out, two_out, x_out, ones, twos, one_t, two_t, table, hot, parts,
                   got_one, sum_one, got_two, piece, x_buf, y_buf, a_buf, hid_ref, x_all, ids, flat, slot,
                   send_sem, recv_sem, one_send, one_recv, two_send, two_recv, line_send, line_recv, hop_send, hop_recv, loc_sem):
    plane = Plane()
    stage = lax.axis_index('pp')
    tp = plane.tp
    stages = last + 1
    moves = ((emb, table), (w_one, ones.at[tp]), (w_two, twos.at[tp]), (one_t, one_out), (two_t, two_out), (hid_ref, hid_out), (x_all, x_out))
    load, own_one, own_two, *saves = [local(src, dst, loc_sem.at[i]) for i, (src, dst) in enumerate(moves)]
    save_one, save_two, save_hid, save_x = saves
    load.start()
    own_one.start()
    own_two.start()
    for peer in plane.rings() + [{'pp': lax.rem(stage + d, stages)} for d in range(1, stages)]:
        signal(peer)

    own_one.wait()
    own_two.wait()
    pl.semaphore_wait(pltpu.get_barrier_semaphore(), 6 + last)
    gather = plane_gather(plane, [(ones, 0, ones.shape[1]), (twos, 0, twos.shape[1])], send_sem, recv_sem)
    next(gather)

    rows, width = table.shape
    group = ids.shape[1]
    unit = piece.shape[0]
    count = group // tokens.shape[1]
    flatten(tokens.at[pl.ds(pl.multiple_of(stage * count, count), count)], ids)
    hot[:] = jnp.where(ids[:] - tp * rows == lax.broadcasted_iota(jnp.int32, hot.shape, 0), 1.0, 0.0).astype(BF16)
    load.wait()
    cut = rows // group * group
    for cols in tiles(width):
        picked = contract(hot[:cut], table[:cut, cols], 0, 0) + contract(hot[cut:], table[cut:, cols], 0, 0)
        parts[:, :, :, cols] = picked.astype(BF16).reshape(*parts.shape[:-1], TILE)
    red = Reduce(plane, parts, got_one, sum_one, got_two, one_send, one_recv, two_send, two_recv)
    for half in BOTH:
        red.begin(half)
    next(gather)
    next(gather)
    red.middle()
    next(gather)
    next(gather)
    for half, total in enumerate(red.end()):
        piece[:, half * (width // 2):(half + 1) * (width // 2)] = total.astype(BF16)

    def line(p):
        return remote(piece, x_buf.at[pl.ds(pl.multiple_of(p * unit, unit), unit)], line_send, line_recv, {'pp': 0})

    @pl.when(stage != 0)
    def _():
        line(stage).start()

    @pl.when(stage == 0)
    def _():
        x_buf[:unit] = piece[:]

    drain(gather)

    blocks, _, cols = ones.shape

    def spare_time():
        @pl.loop(0, blocks)
        def _(k):
            one_t[k] = ones[k].T
            two_t[k] = twos[k].T

        save_one.start()
        save_two.start()
        list_rows(tokens, tp * rows, rows, group, unit, flat, slot, order_out)

    pl.when(stage > 1)(spare_time)
    hop = remote(y_buf, x_buf, hop_send, hop_recv, {'pp': lax.rem(stage + 1, stages)})

    @pl.when(stage == 0)
    def _():
        got = x_buf.at[pl.ds(0, last * unit)]
        remote(got, got, line_send, line_recv, {'pp': last}).wait_recv()

    pl.when(stage > 0)(hop.wait_recv)
    x_act = x_buf[:]
    for k in range(blocks):
        hidden = jnp.dot(x_act, ones[k], preferred_element_type=F32)
        hid_ref[k] = hidden
        a_buf[:, k * cols:(k + 1) * cols] = gelu(hidden).astype(BF16)
    save_hid.start()
    gate = a_buf[:]
    for tile in tiles(width):
        branch = jnp.dot(gate, twos[:, :, tile].reshape(blocks * cols, TILE), preferred_element_type=F32)
        y_buf[:, tile] = (x_buf[:, tile].astype(F32) + branch).astype(BF16)

    pl.when(stage < last)(hop.start)
    y_out[:] = y_buf[:]
    x_all[tp] = x_buf[:]

    @pl.when(stage < SIDE)
    def _():
        steps = plane_gather(plane, [(x_all, 0, x_all.shape[1])], send_sem, recv_sem, base=2)
        next(steps)
        next(steps)
        pl.when(stage <= 1)(spare_time)
        drain(steps)

    save_x.start()
    red.close()

    @pl.when(stage != 0)
    def _():
        line(stage).wait_send()

    pl.when(stage < last)(hop.wait_send)
    for save in saves:
        save.wait()


def norm_of(x):
    wide = x.astype(F32)
    inv_rms = lax.rsqrt(jnp.mean(wide * wide, axis=-1, keepdims=True) + NORM_EPS)
    return inv_rms, wide * inv_rms


class Spread:
    def __init__(self, plane, source, stages, src, out, line_send, line_recv, die_send, die_recv):
        self.plane, self.source, self.stages, self.src, self.out = plane, source, stages, src, out
        self.line_send, self.line_recv, self.die_send, self.die_recv = line_send, line_recv, die_send, die_recv
        self.stage = lax.axis_index('pp')
        self.core = lax.rem(self.stage, 2)
        self.mate = {'pp': self.stage + 1 - 2 * self.core}
        self.rows = out.shape[1] // 2
        self.lo = pl.multiple_of(self.core * self.rows, self.rows)
        self.others = [p for p in range(stages) if p != source]

    def greet(self):
        twin = self.source ^ 1

        @pl.when(self.stage == self.source)
        def _():
            for p in self.others:
                signal({'pp': p})

        @pl.when(self.stage != self.source)
        def _():
            signal({'pp': self.source})

        @pl.when((self.stage != self.source) & (self.stage != twin))
        def _():
            signal(self.mate)

        return jnp.where(self.stage == self.source, len(self.others), jnp.where(self.stage == twin, 1, 2))

    def line(self, p):
        part = pl.ds((p % 2) * self.rows, self.rows)
        return remote(self.src.at[part], self.out.at[self.plane.tp, part], self.line_send, self.line_recv, {'pp': p})

    def send(self):
        for p in self.others:
            self.line(p).start()
        part = pl.ds(self.lo, self.rows)
        self.out[self.plane.tp, part] = self.src[part]

    def arrive(self):
        mine = self.out.at[self.plane.tp, pl.ds(self.lo, self.rows)]
        remote(mine, mine, self.line_recv, self.line_recv, self.mate).wait_recv()

    def on_block(self, a, half, j, k):
        if a == 0:
            size = self.rows // 2
            ref = self.out.at[self.plane.blk(half, HOPS[j], HOPS[k]), pl.ds(self.lo + half * size, size)]
            remote(ref, ref, self.die_send, self.die_recv, self.mate).start()

    def half(self, lo):
        ref = self.out.at[:, pl.ds(lo, self.rows)]
        return remote(ref, ref, self.die_send, self.die_recv, self.mate)

    def finish(self):
        self.half(pl.multiple_of((1 - self.core) * self.rows, self.rows)).wait_recv()

    def close(self):
        self.half(self.lo).wait_send()

        @pl.when(self.stage == self.source)
        def _():
            sent = self.out.at[pl.ds(0, len(self.others)), pl.ds(self.lo, self.rows)]
            remote(sent, sent, self.line_send, self.line_recv, self.mate).wait_send()


def head_kernel(target, stages, middle, chunk, emb, y_ref, labels, x_in, loss_out, g_top, g_out, n_out, x_out,
                table, top, own_x, n_src, n_buf, x_all, lab, g_buf, peak, stat, shared, scale_ref, parts, got_one, sum_one, got_two, piece,
                send_sem, recv_sem, share_send, share_recv, own_send, own_recv, spread_send, spread_recv, die_send, die_recv,
                one_send, one_recv, two_send, two_recv, line_send, line_recv, loc_sem, *e_bufs):
    plane = Plane()
    stage = lax.axis_index('pp')
    tp = plane.tp
    size = shared.shape[1]
    others = [p for p in range(stages) if p != target]
    load = local(emb, table, loc_sem.at[0])
    load.start()
    upper = stage >= middle
    mine = local(x_in.at[tp], x_all.at[tp], loc_sem.at[2])
    pl.when(upper)(mine.start)
    spread = Spread(plane, target, stages, n_src, top, spread_send, spread_recv, die_send, die_recv)
    for d in range(1, size):
        signal({'tp': lax.rem(tp + d, size)})
    extra = spread.greet()
    n_src[:] = norm_of(y_ref[:])[1].astype(BF16)
    group = peak.shape[1]
    unit = group // size
    pl.semaphore_wait(pltpu.get_barrier_semaphore(), size - 1 + extra)

    def own(p):
        return remote(y_ref.at[pl.ds(p * unit, unit)], own_x, own_send, own_recv, {'pp': p})

    @pl.when(stage == target)
    def _():
        spread.send()
        for p in others:
            own(p).start()
        own_x[:] = y_ref[target * unit:(target + 1) * unit]

    pl.when(stage != target)(spread.arrive)
    drain(plane_gather(plane, [(top, spread.lo, spread.rows)], send_sem, recv_sem, spread.on_block))
    spread.finish()
    for p in range(stages):
        n_buf[p * group:(p + 1) * group] = top[:, p * unit:(p + 1) * unit, :].reshape(group, top.shape[2])
    save_n = local(n_buf, n_out, loc_sem.at[1])
    save_n.start()
    load.wait()

    top_plane = stage >= middle + 2
    ways = [(here, plane_gather(plane, [(x_all, 0, x_all.shape[1])], send_sem, recv_sem, base=1)) for here in (top_plane, upper & (stage < middle + 2))]
    pl.when(upper)(mine.wait)
    for here, steps in ways:
        pl.when(here)(functools.partial(next, steps))

    rows, width = table.shape
    flatten(labels, lab)
    lab[:] = lab[:] - tp * rows
    pieces = len(e_bufs)
    pair = e_bufs[0].shape[1]

    def logit_chunk(b, start, count):
        logits = contract(table[pl.ds(start, count), :], n_buf[b * pair:(b + 1) * pair, :], 1, 1)
        e_bufs[b][pl.ds(start, count), :] = logits
        return fold(jnp.max, logits)

    def exp_chunk(b, start, count, top_b, total, hits):
        logits = e_bufs[b][pl.ds(start, count), :]
        label = jnp.concatenate([lab[p:p + 1, :] for p in range(b * pair // group, (b + 1) * pair // group)], axis=1)
        hit = label == start + lax.broadcasted_iota(jnp.int32, logits.shape, 0)
        e = jnp.exp(logits - top_b)
        e_bufs[b][pl.ds(start, count), :] = e
        return total + fold(jnp.sum, e), hits + fold(jnp.sum, jnp.where(hit, logits, 0.0))

    top_b = None
    zero = jnp.zeros((8, pair), F32)
    for b in range(pieces + 1):
        def both(start, count, carry, b=b, top_b=top_b):
            best, total, hits = carry
            if b < pieces:
                best = jnp.maximum(best, logit_chunk(b, start, count))
            if b > 0:
                total, hits = exp_chunk(b - 1, start, count, top_b, total, hits)
            return best, total, hits

        carry = (jnp.full((8, pair), -jnp.inf, F32), zero, zero)
        best, total, hits = lax.fori_loop(0, rows // chunk, lambda c, carry: both(pl.multiple_of(c * chunk, 8), chunk, carry), carry)
        if b > 0:
            lse = top_b + jnp.log(jnp.sum(total, axis=0, keepdims=True))
            hits = jnp.sum(hits, axis=0, keepdims=True)
            for i in range(pair // group):
                p = (b - 1) * (pair // group) + i
                stat[0, p:p + 1, :] = lse[:, i * group:(i + 1) * group]
                stat[1, p:p + 1, :] = hits[:, i * group:(i + 1) * group]
                peak[p:p + 1, :] = top_b[:, i * group:(i + 1) * group]
        if b < pieces:
            top_b = jnp.max(best, axis=0, keepdims=True)
        if b in (2, 3):
            pl.when(top_plane)(functools.partial(next, ways[0][1]))
        if b == pieces - 1:
            pl.when(ways[1][0])(functools.partial(next, ways[1][1]))

    def msg(d, kind):
        return remote(stat.at[kind], shared.at[kind, tp], share_send.at[kind], share_recv.at[kind], {'tp': lax.rem(tp + d, size)})

    for kind in BOTH:
        for d in range(1, size):
            msg(d, kind).start()
        shared[kind, tp] = stat[kind]

    def shares(kind):
        ref = shared.at[kind, pl.ds(0, size - 1)]
        return remote(ref, ref, share_send.at[kind], share_recv.at[kind], {'tp': plane.at(1, 0)})

    shares(0).wait_recv()
    every = shared[0]
    most = jnp.max(every, axis=0)
    log_norm = most + jnp.log(jnp.sum(jnp.exp(every - most[None]), axis=0))
    scale_ref[:] = jnp.exp(peak[:] - log_norm)

    def grad_block(p, slot):
        e_ref = e_bufs[p // (pair // group)]
        col = p % (pair // group) * group

        def part(start, count):
            e = e_ref[pl.ds(start, count), col:col + group]
            hit = lab[p:p + 1, :] == start + lax.broadcasted_iota(jnp.int32, e.shape, 0)
            g_buf[slot, pl.ds(start, count), :] = (e * scale_ref[p:p + 1, :] - jnp.where(hit, 1.0, 0.0)).astype(BF16)

        @pl.loop(0, rows // chunk)
        def _(c):
            part(pl.multiple_of(c * chunk, 8), chunk)

    def save(p):
        slot = 1 + p % 2
        return local(g_buf.at[slot], g_out.at[:, p * group:(p + 1) * group], loc_sem.at[2 + slot])

    for p in range(stages):
        pl.when(stage == p)(functools.partial(grad_block, p, 0))
    cut = rows // group * group
    red = Reduce(plane, parts, got_one, sum_one, got_two, one_send, one_recv, two_send, two_recv)
    mine_g = g_buf.at[0]
    half = width // 2
    for cols in tiles(width):
        back = contract(mine_g[:cut, :], table[:cut, cols], 0, 0) + contract(mine_g[cut:, :], table[cut:, cols], 0, 0)
        parts[:, :, :, cols] = back.reshape(*parts.shape[:-1], TILE)
        if cols.stop % half == 0:
            red.begin(cols.start // half)
    for p in range(stages):
        if p >= 2:
            save(p - 2).wait()
        grad_block(p, 1 + p % 2)
        save(p).start()
    red.middle()
    sums = red.end()

    @pl.when(stage != target)
    def _():
        remote(own_x, own_x, own_recv, own_recv, spread.mate).wait_recv()

    inv_rms, normed = norm_of(own_x[:])
    mean = (jnp.sum(normed[:, :half] * sums[0], axis=-1, keepdims=True) + jnp.sum(normed[:, half:] * sums[1], axis=-1, keepdims=True)) / width
    for h in BOTH:
        piece[:, h * half:(h + 1) * half] = (inv_rms * (sums[h] - normed[:, h * half:(h + 1) * half] * mean)).astype(BF16)

    def line(p):
        return remote(piece, g_top.at[p], line_send, line_recv, {'pp': target})

    @pl.when(stage != target)
    def _():
        line(stage).start()

    for here, steps in ways:
        pl.when(here)(functools.partial(drain, steps))

    save_x = local(x_all, x_out, loc_sem.at[2])
    pl.when(upper)(save_x.start)

    @pl.when(stage == target)
    def _():
        g_top[target] = piece[:]
        got = g_top.at[pl.ds(0, len(others))]
        remote(got, got, line_send, line_recv, spread.mate).wait_recv()

    red.close()
    pl.when(upper)(save_x.wait)
    shares(1).wait_recv()
    loss_out[:] = jnp.sum(log_norm - jnp.sum(shared[1], axis=0), keepdims=True) / (stages * group)
    for kind in BOTH:
        shares(kind).wait_send()
    save_n.wait()
    save(stages - 2).wait()
    save(stages - 1).wait()
    spread.close()

    @pl.when(stage == target)
    def _():
        sent = y_ref.at[pl.ds(0, len(others) * unit)]
        remote(sent, sent, own_send, own_recv, spread.mate).wait_send()

    @pl.when(stage != target)
    def _():
        line(stage).wait_send()


def backward_kernel(last, middle, chunk, g_top, hid_in, one_all, two_all, g_all, n_all, x_in, x_mid, w_one, w_two, de_buf, dx_all, grad_one, grad_two,
                    ones, twos, slope_ref, g_buf, n_buf, x_all, w_one_buf, w_two_buf, dy_all, dy_buf, dx_buf, d_buf,
                    send_sem, recv_sem, spread_send, spread_recv, die_send, die_recv, hop_send, hop_recv, go_sem, ready_sem, g_sem, loc_sem):
    plane = Plane()
    stage = lax.axis_index('pp')
    stages = last + 1
    blocks, cols, width = one_all.shape
    pairs = ((hid_in, slope_ref), (two_all, twos), (one_all, ones), (n_all, n_buf), (w_one, w_one_buf), (w_two, w_two_buf))
    loads = [local(src, dst, loc_sem.at[i]) for i, (src, dst) in enumerate(pairs)]
    lower = stage < middle
    load_x = [local(src, x_all, loc_sem.at[6]) for src in (x_in, x_mid)]

    def load_rest(at):
        for load in loads[3:] + [load_x[at]]:
            load.start()

    for load in loads[:3]:
        load.start()
    pl.when(lower)(functools.partial(load_rest, 0))
    spread = Spread(plane, 0, stages, dx_buf, dx_all, spread_send, spread_recv, die_send, die_recv)
    near = plane.near()
    for peer in near:
        signal(peer)
    extra = spread.greet()
    before = {'pp': lax.rem(stage + last, stages)}
    pl.when(stage > 0)(functools.partial(signal, before))
    hop = remote(dx_buf, dy_buf, hop_send, hop_recv, before)
    rows = de_buf.shape[0]
    pieces = -(-rows // chunk)

    def piece_at(c):
        return pl.ds(pl.multiple_of(jnp.minimum(c * chunk, rows - chunk), 8), chunk)

    def fetch(c):
        slot = lax.rem(c, 2)
        return local(g_all.at[piece_at(c)], g_buf.at[slot], g_sem.at[slot])

    def table(lo, hi):
        if lo == 0:
            fetch(0).start()
            loads[3].wait()

        @pl.loop(lo, hi)
        def _(c):
            @pl.when(c < pieces - 1)
            def _():
                fetch(c + 1).start()

            fetch(c).wait()
            de_buf[piece_at(c), :] = jnp.dot(g_buf[lax.rem(c, 2)], n_buf[:], preferred_element_type=F32)

    pl.when(lower)(functools.partial(table, 0, pieces))
    pl.semaphore_wait(pltpu.get_barrier_semaphore(), len(near) + extra + jnp.where(stage < last, 1, 0))

    @pl.when(stage < last)
    def _():
        pl.semaphore_signal(ready_sem, inc=1, device_id={'pp': lax.rem(stage + 1, stages)}, device_id_type=MESH)

    loads[0].wait()
    for k in range(blocks):
        slope_ref[k] = gelu_slope(slope_ref[k])
    loads[1].wait()

    @pl.when(stage == last)
    def _():
        dy_buf[:] = g_top[:]

    pl.when(stage < last)(hop.wait_recv)
    dy_all[plane.tp] = dy_buf[:]
    whole = (dy_all, 0, dy_all.shape[1])
    part = (dx_all, spread.lo, spread.rows)

    def dy_steps(begun):
        return plane_gather(plane, [whole], send_sem, recv_sem, base=1, begun=begun)

    @pl.when(stage <= 1)
    def _():
        next(dy_steps(False))

    grad_y = dy_buf[:]
    for k in range(blocks):
        grad_gate = jnp.dot(grad_y, twos[k], preferred_element_type=F32)
        d_buf[:, k * cols:(k + 1) * cols] = (slope_ref[k] * grad_gate).astype(BF16)
    loads[2].wait()
    grad_hidden = d_buf[:]
    for tile in tiles(width):
        back = jnp.dot(grad_hidden, ones[:, :, tile].reshape(blocks * cols, TILE), preferred_element_type=F32)
        dx_buf[:, tile] = (dy_buf[:, tile].astype(F32) + back).astype(BF16)

    @pl.when(stage > 0)
    def _():
        pl.semaphore_wait(ready_sem, 1)
        hop.start()

    pl.when(stage == 0)(spread.send)
    pl.when(jnp.logical_not(lower))(functools.partial(load_rest, 1))
    for load in loads[4:]:
        load.wait()
    load_x[0].wait()

    grad_one[:] = jnp.zeros_like(grad_one)
    grad_two[:] = jnp.zeros_like(grad_two)

    def weights(lo, hi):
        step = SIDE

        @pl.loop(lo, hi)
        def _(c):
            part = pl.ds(c * step, step)
            x_act = x_all[part].reshape(step * x_all.shape[1], width)
            grad_y = dy_all[part].reshape(step * x_all.shape[1], width)
            hidden = jnp.dot(x_act, w_one_buf[:], preferred_element_type=F32)
            grad_gate = contract(grad_y, w_two_buf[:], 1, 1)
            grad_hidden = (gelu_slope(hidden) * grad_gate).astype(BF16)
            grad_one[:] += contract(x_act, grad_hidden, 0, 0)
            grad_two[:] += contract(gelu(hidden).astype(BF16), grad_y, 0, 0)

    def dx_steps():
        return plane_gather(plane, [part], send_sem, recv_sem, spread.on_block)

    @pl.when(stage > 1)
    def _():
        hop.wait_send()

        @pl.when(spread.core == 0)
        def _():
            pl.semaphore_signal(go_sem, inc=1, device_id=spread.mate, device_id_type=MESH)

        @pl.when(spread.core == 1)
        def _():
            pl.semaphore_wait(go_sem, 1)

        next(dy_steps(False))

    @pl.when(jnp.logical_not(lower))
    def _():
        steps = dy_steps(True)
        for lo in range(0, pieces, 3):
            next(steps)
            table(lo, min(lo + 3, pieces))
            next(steps)
        drain(steps)

    planes = [(stage <= 1, 'dxddxdxdxdx', 'xx'), ((stage > 1) & lower, 'dddxdxdxdx', 'xxx')]
    runs = []
    for here, order, rest in planes:
        steps = {'d': dy_steps(True), 'x': dx_steps()}

        def arrived(order=order, steps=steps):
            for i, kind in enumerate(order):
                if kind == 'x' and 'x' not in order[:i]:
                    pl.when(stage > 0)(spread.arrive)
                next(steps[kind])
            drain(steps['d'])

        def onward(rest=rest, steps=steps):
            for kind in rest:
                next(steps[kind])

        pl.when(here)(arrived)
        runs.append((here, onward, functools.partial(drain, steps['x'])))

    weights(0, 2)
    for here, onward, _ in runs:
        pl.when(here)(onward)
    weights(2, SIDE)
    for here, _, finish in runs:
        pl.when(here)(finish)

    @pl.when(jnp.logical_not(lower))
    def _():
        spread.arrive()
        drain(dx_steps())

    spread.finish()
    spread.close()

    pl.when(stage == 1)(hop.wait_send)


def add_kernel(pieces, order, dx_ref, de_ref, one_ref, two_ref, de_out, table_out, one_out, two_out, wide, sem):
    saves = [local(one_ref, one_out, sem.at[0]), local(two_ref, two_out, sem.at[1])]
    for save in saves:
        save.start()
    wide[:] = dx_ref[:].astype(F32)

    @pl.loop(0, order[2, 0])
    def _(j):
        row = pl.ds(order[1, j], 1)
        de_out[row, :] = de_out[row, :] + wide[pl.ds(order[0, j], 1), :]

    rows = de_ref.shape[0]
    size = -(-rows // (8 * pieces)) * 8
    for c in range(pieces):
        part = pl.ds(c * size, min(size, rows - c * size))
        saves.append(local(de_out.at[part], table_out.at[part], sem.at[2 + c]))
        saves[-1].start()
    for save in saves:
        save.wait()


def vmem():
    return pl.BlockSpec(memory_space=pltpu.VMEM)


def anywhere():
    return pl.BlockSpec(memory_space=pl.ANY)


def params(cid, mib):
    return pltpu.CompilerParams(collective_id=cid, has_side_effects=True, vmem_limit_bytes=mib << 20)


DMA = pltpu.SemaphoreType.DMA


def solution(mesh):
    pp_size = mesh.shape['pp']
    tp_size = mesh.shape['tp']
    last = pp_size - 1

    def device_fn(tokens, labels, emb_table, w_in, w_out):
        num_tokens = tokens.shape[0] * tokens.shape[1]
        vocab_rows, width = emb_table.shape
        w_one, w_two = w_in[0], w_out[0]
        cols = w_one.shape[1]
        unit = num_tokens // (pp_size * tp_size)
        block = pp_size * unit
        group = tp_size * unit
        half = width // 2
        chunk = vocab_rows // 3
        step = 512
        pair = 2 * group
        shape = jax.ShapeDtypeStruct
        VM = pltpu.VMEM

        def reduce_scratch(dtype):
            return [VM((SIDE, SIDE, unit, width), dtype), VM((6, SIDE, unit, half), dtype), VM((2, SIDE, unit, half), dtype), VM((6, unit, half), dtype), VM((unit, width), BF16)]

        reduce_sems = [DMA, DMA((2,)), DMA, DMA((2,)), DMA, DMA]
        many = shape((tp_size, block, width), BF16)
        many_buf = VM((tp_size, block, width), BF16)
        two_sums = 2 * SLOTS

        y_act, order, hidden, one_t, two_t, x_all = pl.pallas_call(
            functools.partial(forward_kernel, last),
            out_shape=(shape((block, width), BF16), shape((3, num_tokens), jnp.int32), shape((tp_size, block, cols), F32), shape((tp_size, cols, width), BF16), shape((tp_size, width, cols), BF16), many),
            in_specs=[vmem()] + [anywhere()] * 3,
            out_specs=[vmem()] * 2 + [anywhere()] * 4,
            scratch_shapes=[VM((tp_size, width, cols), BF16), VM((tp_size, cols, width), BF16), VM((tp_size, cols, width), BF16), VM((tp_size, width, cols), BF16),
                            VM((vocab_rows, width), BF16), VM((vocab_rows, group), BF16), *reduce_scratch(BF16),
                            VM((block, width), BF16), VM((block, width), BF16), VM((block, tp_size * cols), BF16), VM((tp_size, block, cols), F32), many_buf, VM((1, group), jnp.int32),
                            VM((num_tokens // 128, 128), jnp.int32), VM((2, num_tokens), jnp.int32),
                            DMA((3,)), DMA((3 * two_sums,)), *reduce_sems, DMA, DMA, DMA((7,))],
            compiler_params=params(1, 58), name='forward_chain',
        )(tokens, emb_table, w_one, w_two)

        spread_sems = [DMA, DMA, DMA, DMA]
        middle = pp_size // 2
        loss, g_top, g_all, n_all, x_mid = pl.pallas_call(
            functools.partial(head_kernel, last, pp_size, middle, chunk),
            out_shape=(shape((1, 1), F32), shape((pp_size, unit, width), BF16), shape((vocab_rows, num_tokens), BF16), shape((num_tokens, width), BF16), many),
            in_specs=[anywhere(), vmem(), vmem(), anywhere()],
            out_specs=[vmem()] * 2 + [anywhere()] * 3,
            scratch_shapes=[VM((vocab_rows, width), BF16), many_buf, VM((unit, width), BF16), VM((block, width), BF16), VM((num_tokens, width), BF16),
                            many_buf, VM((pp_size, group), jnp.int32), VM((3, vocab_rows, group), BF16),
                            VM((pp_size, group), F32), VM((2, pp_size, group), F32), VM((2, tp_size, pp_size, group), F32), VM((pp_size, group), F32), *reduce_scratch(F32),
                            DMA((2,)), DMA((2 * two_sums,)), DMA((2,)), DMA((2,)), DMA, DMA, *spread_sems, *reduce_sems, DMA((5,)),
                            *[VM((vocab_rows, pair), F32) for _ in range(num_tokens // pair)]],
            compiler_params=params(2, 60), name='head',
        )(emb_table, y_act, labels, x_all)

        de_head, dx_first, grad_one, grad_two = pl.pallas_call(
            functools.partial(backward_kernel, last, middle, step),
            out_shape=(VM((vocab_rows, width), F32), many_buf, VM((width, cols), F32), VM((cols, width), F32)),
            in_specs=[vmem()] + [anywhere()] * 9, out_specs=[vmem()] * 4,
            scratch_shapes=[VM((tp_size, cols, width), BF16), VM((tp_size, width, cols), BF16), VM((tp_size, block, cols), F32), VM((2, step, num_tokens), BF16), VM((num_tokens, width), BF16),
                            many_buf, VM((width, cols), BF16), VM((cols, width), BF16), many_buf,
                            VM((block, width), BF16), VM((block, width), BF16), VM((block, tp_size * cols), BF16),
                            DMA((3,)), DMA((3 * two_sums,)), *spread_sems, DMA, DMA, pltpu.SemaphoreType.REGULAR, pltpu.SemaphoreType.REGULAR, DMA((2,)), DMA((7,))],
            compiler_params=params(3, 44), name='backward_chain',
        )(g_top.reshape(block, width), hidden, one_t, two_t, g_all, n_all, x_all, x_mid, w_one, w_two)

        smem = pl.BlockSpec(memory_space=pltpu.SMEM)
        _, grad_table, grad_one, grad_two = pl.pallas_call(
            functools.partial(add_kernel, 12),
            out_shape=(VM((vocab_rows, width), F32), shape((vocab_rows, width), F32), shape((width, cols), F32), shape((cols, width), F32)),
            in_specs=[smem] + [vmem()] * 4, out_specs=[vmem()] + [anywhere()] * 3,
            scratch_shapes=[VM((num_tokens, width), F32), DMA((14,))], input_output_aliases={2: 0},
            compiler_params=pltpu.CompilerParams(vmem_limit_bytes=24 << 20), name='add_rows',
        )(order, dx_first.reshape(num_tokens, width), de_head, grad_one, grad_two)
        return loss.reshape(1), grad_one[None], grad_two[None], grad_table

    return jax.shard_map(device_fn, mesh=mesh, in_specs=(P('dp', None), P('dp', None), P('tp', None), P('pp', None, 'tp'), P('pp', 'tp', None)), out_specs=(P('dp'), P(('dp', 'pp'), None, 'tp'), P(('dp', 'pp'), 'tp', None), P(('dp', 'tp'), None)), check_vma=False)
```

profile of v0, /device:TPU:1, one launch (start us, length us, event | category | flops | bytes accessed | tf_op | source)
XLA Modules:
  0.0 313.5 jit_solution(7210736237250211851)
XLA Ops:
  0.6 133.1 %forward_chain.1 = (bf16[128,1024]{1,0:T(8,128)(2,1)}, s32[3,2048]{1,0:T(4,128)}, f32[16,128,256]{2,1,0:T(8,128)}, bf16[16,256,1024]{2,1,0:T(8,128)(2,1)}, bf16[...) custom-call(s32[32,64]{1,0:T(8,128)} %tokens.1, bf16[3144,1024]{1,0:T(8,128)(2,1)} %emb.3, ...), custom_call_target="tpu_custom_call" | custom-call | tf_op jit(solution)/shard_map/forward_chain/pallas_call | solution.py:873
  133.7 75.9 %head.1 = (f32[1,1]{1,0:T(1,128)}, bf16[8,16,1024]{2,1,0:T(8,128)(2,1)}, bf16[3144,2048]{1,0:T(8,128)(2,1)}, bf16[2048,1024]{1,0:T(8,128)(2,1)}, bf16[16,128,1024]{2,1,0:T(8,128)(2,1)}) custom-call(bf16[3144,1024]{1,0:T(8,128)(2,1)} %emb.3, bf16[128,1024]{1,0:T(8,128)(2,1)} %get-tuple-element.22.y_ref, s32[32,64]{1,0:T(8,128)} %labels.1, ...), custom_call_target="tpu_custom_call" | custom-call | tf_op jit(solution)/shard_map/head/pallas_call | solution.py:888
  209.7 0.0 copy-start
  209.7 94.2 %backward_chain.1 = (f32[3144,1024]{1,0:T(8,128)S(1)}, bf16[16,128,1024]{2,1,0:T(8,128)(2,1)S(1)}, f32[1024,256]{1,0:T(8,128)S(1)}, f32[256,1024]{1,0:T(8,128)S(1)}) custom-call(bf16[128,1024]{1,0:T(8,128)(2,1)} %bitcast.12, f32[16,128,256]{2,1,0:T(8,128)} %get-tuple-element.27.hid_in, bf16[16,256,1024]{2,1,0:T(8,128)(2,1)} %get-tuple-element.28.one_all, ...), custom_call_target="tpu_custom_call" | custom-call | tf_op jit(solution)/shard_map/backward_chain/pallas_call | solution.py:901
  303.9 0.0 copy-done
  303.9 7.8 %add_rows.1 = (f32[3144,1024]{1,0:T(8,128)S(1)}, f32[3144,1024]{1,0:T(8,128)}, f32[1024,256]{1,0:T(8,128)}, f32[256,1024]{1,0:T(8,128)}) custom-call(s32[3,2048]{1,0:T(4,128)S(1)} %copy-done, bf16[2048,1024]{1,0:T(8,128)(2,1)S(1)} %bitcast.7, f32[3144,1024]{1,0:T(8,128)S(1)} %get-tuple-element.34.de_ref, ...), custom_call_target="tpu_custom_call", output_to_operand_aliasing={{0}: (2, {})} | custom-call | tf_op jit(solution)/shard_map/add_rows/pallas_call | solution.py:913
Async XLA Ops:
  209.7 94.2 %copy-start = (s32[3,2048]{1,0:T(4,128)S(1)}, s32[3,2048]{1,0:T(4,128)}, u32[]{:S(2)}) copy-start(s32[3,2048]{1,0:T(4,128)} %get-tuple-element.25.order) | copy-start | bytes 73732
where the time goes:
time: 314 us; the launch traced here: 313 us
  Pallas kernels  311 us (99%)
    pallas_call x1, Pallas kernels, device_fn(): pl.pallas_call(functools.partial(forward_kernel, last), out_shape=(shape(...  133 us
    pallas_call x1, Pallas kernels, device_fn(): pl.pallas_call(functools.partial(backward_kernel, last, middle, step), ou...  94.2 us
    pallas_call x1, Pallas kernels, device_fn(): pl.pallas_call(functools.partial(head_kernel, last, pp_size, middle, chun...  75.9 us
    pallas_call x1, Pallas kernels, device_fn(): pl.pallas_call(functools.partial(add_kernel, 12), out_shape=(VM((vocab_ro...  7.85 us

commit v1 on v0

--- a/solution.py
+++ b/solution.py
@@ -16,8 +16,16 @@
 ROOT = 0.7978845608028654
 
 
-def contract(lhs, rhs, lhs_dim, rhs_dim):
-    return lax.dot_general(lhs, rhs, (((lhs_dim,), (rhs_dim,)), ((), ())), preferred_element_type=F32)
+def dot(lhs, rhs):
+    return jnp.dot(lhs, rhs, preferred_element_type=F32)
+
+
+def rows_dot(lhs, rhs):
+    return lax.dot_general(lhs, rhs, (((0,), (0,)), ((), ())), preferred_element_type=F32)
+
+
+def cols_dot(lhs, rhs):
+    return lax.dot_general(lhs, rhs, (((1,), (1,)), ((), ())), preferred_element_type=F32)
 
 
 def gelu(h):
@@ -218,7 +226,7 @@
     mine = (row >= 0) & (row < rows)
     upper = lax.broadcasted_iota(jnp.int32, (lanes, lanes), 0) <= lax.broadcasted_iota(jnp.int32, (lanes, lanes), 1)
     ones = [jnp.where(mask, 1.0, 0.0).astype(BF16) for mask in (mine, upper)]
-    seen = jnp.dot(*ones, preferred_element_type=F32)
+    seen = dot(*ones)
     total = jnp.zeros((1, 1), F32)
     for r in range(lines):
         line = slice(r, r + 1)
@@ -237,7 +245,7 @@
     def _(c):
         start = pl.multiple_of(c * group, group)
         pick = jnp.where(slot[:1, :] == start + lax.broadcasted_iota(jnp.int32, (group, count), 0), 1.0, 0.0).astype(BF16)
-        found = contract(values, pick, 1, 1)
+        found = cols_dot(values, pick)
         for i in BOTH:
             out[i:i + 1, pl.ds(start, group)] = (found[2 * i:2 * i + 1] * 256.0 + found[2 * i + 1:2 * i + 2]).astype(jnp.int32)
 
@@ -246,11 +254,12 @@
 
 def forward_kernel(last, tokens, emb, w_one, w_two, y_out, order_out, hid_out, one_out, two_out, x_out, ones, twos, one_t, two_t, table, hot, parts,
                    got_one, sum_one, got_two, piece, x_buf, y_buf, a_buf, hid_ref, x_all, ids, flat, slot,
-                   send_sem, recv_sem, one_send, one_recv, two_send, two_recv, line_send, line_recv, hop_send, hop_recv, loc_sem):
+                   send_sem, recv_sem, one_send, one_recv, two_send, two_recv, line_send, line_recv, hop_send, hop_recv, lead_sem, loc_sem):
     plane = Plane()
     stage = lax.axis_index('pp')
     tp = plane.tp
     stages = last + 1
+    core = lax.rem(stage, 2)
     moves = ((emb, table), (w_one, ones.at[tp]), (w_two, twos.at[tp]), (one_t, one_out), (two_t, two_out), (hid_ref, hid_out), (x_all, x_out))
     load, own_one, own_two, *saves = [local(src, dst, loc_sem.at[i]) for i, (src, dst) in enumerate(moves)]
     save_one, save_two, save_hid, save_x = saves
@@ -263,8 +272,12 @@
     own_one.wait()
     own_two.wait()
     pl.semaphore_wait(pltpu.get_barrier_semaphore(), 6 + last)
-    gather = plane_gather(plane, [(ones, 0, ones.shape[1]), (twos, 0, twos.shape[1])], send_sem, recv_sem)
-    next(gather)
+    def weight_steps(begun=False):
+        return plane_gather(plane, [(ones, 0, ones.shape[1]), (twos, 0, twos.shape[1])], send_sem, recv_sem, begun=begun)
+
+    @pl.when(core == 0)
+    def _():
+        next(weight_steps())
 
     rows, width = table.shape
     group = ids.shape[1]
@@ -275,12 +288,24 @@
     load.wait()
     cut = rows // group * group
     for cols in tiles(width):
-        picked = contract(hot[:cut], table[:cut, cols], 0, 0) + contract(hot[cut:], table[cut:, cols], 0, 0)
+        picked = rows_dot(hot[:cut], table[:cut, cols]) + rows_dot(hot[cut:], table[cut:, cols])
         parts[:, :, :, cols] = picked.astype(BF16).reshape(*parts.shape[:-1], TILE)
     red = Reduce(plane, parts, got_one, sum_one, got_two, one_send, one_recv, two_send, two_recv)
     for half in BOTH:
         red.begin(half)
+
+    @pl.when(core == 1)
+    def _():
+        pl.semaphore_wait(lead_sem, 1)
+        next(weight_steps())
+
+    gather = weight_steps(True)
     next(gather)
+
+    @pl.when(core == 0)
+    def _():
+        pl.semaphore_signal(lead_sem, inc=1, device_id={'pp': stage + 1}, device_id_type=MESH)
+
     next(gather)
     red.middle()
     next(gather)
@@ -301,6 +326,10 @@
 
     drain(gather)
 
+    @pl.when(stage == 1)
+    def _():
+        pl.semaphore_signal(lead_sem, inc=1, device_id={'pp': 0}, device_id_type=MESH)
+
     blocks, _, cols = ones.shape
 
     def spare_time():
@@ -324,13 +353,13 @@
     pl.when(stage > 0)(hop.wait_recv)
     x_act = x_buf[:]
     for k in range(blocks):
-        hidden = jnp.dot(x_act, ones[k], preferred_element_type=F32)
+        hidden = dot(x_act, ones[k])
         hid_ref[k] = hidden
         a_buf[:, k * cols:(k + 1) * cols] = gelu(hidden).astype(BF16)
     save_hid.start()
     gate = a_buf[:]
     for tile in tiles(width):
-        branch = jnp.dot(gate, twos[:, :, tile].reshape(blocks * cols, TILE), preferred_element_type=F32)
+        branch = dot(gate, twos[:, :, tile].reshape(blocks * cols, TILE))
         y_buf[:, tile] = (x_buf[:, tile].astype(F32) + branch).astype(BF16)
 
     pl.when(stage < last)(hop.start)
@@ -339,13 +368,18 @@
 
     @pl.when(stage < SIDE)
     def _():
+        pl.when(stage <= 1)(spare_time)
+
+        @pl.when(stage == 0)
+        def _():
+            pl.semaphore_wait(lead_sem, 1)
+
         steps = plane_gather(plane, [(x_all, 0, x_all.shape[1])], send_sem, recv_sem, base=2)
-        next(steps)
-        next(steps)
-        pl.when(stage <= 1)(spare_time)
         drain(steps)
 
-    save_x.start()
+    own_save = local(x_all.at[tp], x_out.at[tp], loc_sem.at[6])
+    pl.when(stage < SIDE)(save_x.start)
+    pl.when(stage >= SIDE)(own_save.start)
     red.close()
 
     @pl.when(stage != 0)
@@ -353,8 +387,10 @@
         line(stage).wait_send()
 
     pl.when(stage < last)(hop.wait_send)
-    for save in saves:
+    for save in saves[:-1]:
         save.wait()
+    pl.when(stage < SIDE)(save_x.wait)
+    pl.when(stage >= SIDE)(own_save.wait)
 
 
 def norm_of(x):
@@ -374,23 +410,21 @@
         self.lo = pl.multiple_of(self.core * self.rows, self.rows)
         self.others = [p for p in range(stages) if p != source]
 
-    def greet(self):
-        twin = self.source ^ 1
-
-        @pl.when(self.stage == self.source)
+    def greet(self, back):
+        source = self.stage == self.source
+        twin = self.stage == self.source ^ 1
+
+        @pl.when(source)
         def _():
-            for p in self.others:
+            for p in self.others if back else [self.source ^ 1]:
                 signal({'pp': p})
 
-        @pl.when(self.stage != self.source)
+        @pl.when(jnp.logical_not(source))
         def _():
             signal({'pp': self.source})
 
-        @pl.when((self.stage != self.source) & (self.stage != twin))
-        def _():
-            signal(self.mate)
-
-        return jnp.where(self.stage == self.source, len(self.others), jnp.where(self.stage == twin, 1, 2))
+        pl.when(jnp.logical_not(source | twin))(functools.partial(signal, self.mate))
+        return jnp.where(source, len(self.others), jnp.where(twin, 1, 1 + back))
 
     def line(self, p):
         part = pl.ds((p % 2) * self.rows, self.rows)
@@ -428,8 +462,8 @@
             remote(sent, sent, self.line_send, self.line_recv, self.mate).wait_send()
 
 
-def head_kernel(target, stages, middle, chunk, emb, y_ref, labels, x_in, loss_out, g_top, g_out, n_out, x_out,
-                table, top, own_x, n_src, n_buf, x_all, lab, g_buf, peak, stat, shared, scale_ref, parts, got_one, sum_one, got_two, piece,
+def head_kernel(target, stages, chunk, emb, y_ref, labels, loss_out, g_top, g_out, n_out,
+                table, top, own_x, n_src, n_buf, lab, g_buf, peak, stat, shared, scale_ref, parts, got_one, sum_one, got_two, piece,
                 send_sem, recv_sem, share_send, share_recv, own_send, own_recv, spread_send, spread_recv, die_send, die_recv,
                 one_send, one_recv, two_send, two_recv, line_send, line_recv, loc_sem, *e_bufs):
     plane = Plane()
@@ -439,15 +473,12 @@
     others = [p for p in range(stages) if p != target]
     load = local(emb, table, loc_sem.at[0])
     load.start()
-    upper = stage >= middle
-    mine = local(x_in.at[tp], x_all.at[tp], loc_sem.at[2])
-    pl.when(upper)(mine.start)
     spread = Spread(plane, target, stages, n_src, top, spread_send, spread_recv, die_send, die_recv)
     for d in range(1, size):
         signal({'tp': lax.rem(tp + d, size)})
-    extra = spread.greet()
+    extra = spread.greet(1)
     n_src[:] = norm_of(y_ref[:])[1].astype(BF16)
-    group = peak.shape[1]
+    each, group = peak.shape[1:]
     unit = group // size
     pl.semaphore_wait(pltpu.get_barrier_semaphore(), size - 1 + extra)
 
@@ -470,111 +501,130 @@
     save_n.start()
     load.wait()
 
-    top_plane = stage >= middle + 2
-    ways = [(here, plane_gather(plane, [(x_all, 0, x_all.shape[1])], send_sem, recv_sem, base=1)) for here in (top_plane, upper & (stage < middle + 2))]
-    pl.when(upper)(mine.wait)
-    for here, steps in ways:
-        pl.when(here)(functools.partial(next, steps))
-
     rows, width = table.shape
     flatten(labels, lab)
     lab[:] = lab[:] - tp * rows
     pieces = len(e_bufs)
-    pair = e_bufs[0].shape[1]
-
-    def logit_chunk(b, start, count):
-        logits = contract(table[pl.ds(start, count), :], n_buf[b * pair:(b + 1) * pair, :], 1, 1)
-        e_bufs[b][pl.ds(start, count), :] = logits
+    pair = each * group
+
+    def group_at(b, i):
+        return lax.rem(stage // each + b, pieces) * each + i
+
+    def label_of(p):
+        return lab[pl.ds(p, 1), :]
+
+    def down(value, start):
+        return start + lax.broadcasted_iota(jnp.int32, value.shape, 0)
+
+    def logit_chunk(b, start):
+        tokens = n_buf[pl.ds(pl.multiple_of(group_at(b, 0) * group, pair), pair), :]
+        logits = cols_dot(table[pl.ds(start, chunk), :], tokens)
+        e_bufs[b][pl.ds(start, chunk), :] = logits
         return fold(jnp.max, logits)
 
-    def exp_chunk(b, start, count, top_b, total, hits):
-        logits = e_bufs[b][pl.ds(start, count), :]
-        label = jnp.concatenate([lab[p:p + 1, :] for p in range(b * pair // group, (b + 1) * pair // group)], axis=1)
-        hit = label == start + lax.broadcasted_iota(jnp.int32, logits.shape, 0)
+    def exp_chunk(b, start, label, top_b, total, hits):
+        logits = e_bufs[b][pl.ds(start, chunk), :]
         e = jnp.exp(logits - top_b)
-        e_bufs[b][pl.ds(start, count), :] = e
-        return total + fold(jnp.sum, e), hits + fold(jnp.sum, jnp.where(hit, logits, 0.0))
-
-    top_b = None
+        e_bufs[b][pl.ds(start, chunk), :] = e
+        return total + fold(jnp.sum, e), hits + fold(jnp.sum, jnp.where(label == down(logits, start), logits, 0.0))
+
+    def chunks(body, carry):
+        return lax.fori_loop(0, rows // chunk, lambda c, carry: body(pl.multiple_of(c * chunk, 8), carry), carry)
+
+    def msg(d, k):
+        some = pl.ds(k, 1 + k * (pieces - 2))
+        return remote(stat.at[some], shared.at[some, tp], share_send.at[k], share_recv.at[k], {'tp': lax.rem(tp + d, size)})
+
+    def shares(k):
+        ref = shared.at[pl.ds(k, 1 + k * (pieces - 2)), pl.ds(0, size - 1)]
+        return remote(ref, ref, share_send.at[k], share_recv.at[k], {'tp': plane.at(1, 0)})
+
+    def share(k):
+        for d in range(1, size):
+            msg(d, k).start()
+
+    losses = []
+
+    def normalise(k):
+        shares(k).wait_recv()
+        for b in (range(1, pieces) if k else range(1)):
+            every = shared[b, :, 0]
+            most = jnp.max(every, axis=0)
+            log_norm = most + jnp.log(jnp.sum(jnp.exp(every - most[None]), axis=0))
+            losses.append(jnp.sum(log_norm - jnp.sum(shared[b, :, 1], axis=0), keepdims=True))
+            scale_ref[b] = jnp.exp(peak[b] - log_norm)
+
+    def grad_block(b, i, slot):
+        cols = pl.ds(pl.multiple_of(i * group, group), group)
+        label = label_of(group_at(b, i))
+        factor = scale_ref[b, pl.ds(i, 1), :]
+
+        def part(start, _):
+            e = e_bufs[b][pl.ds(start, chunk), cols]
+            hit = label == down(e, start)
+            g_buf[slot, pl.ds(start, chunk), :] = (e * factor - jnp.where(hit, 1.0, 0.0)).astype(BF16)
+
+        chunks(part, None)
+
+    def save(k):
+        slot = 1 + k % 2
+        at = pl.multiple_of(group_at(k // each, k % each) * group, group)
+        return local(g_buf.at[slot], g_out.at[:, pl.ds(at, group)], loc_sem.at[2 + slot])
+
+    def gradient(k):
+        if k >= 2:
+            save(k - 2).wait()
+        grad_block(k // each, k % each, 1 + k % 2)
+        save(k).start()
+
+    cut = rows // group * group
+    half = width // 2
+    red = Reduce(plane, parts, got_one, sum_one, got_two, one_send, one_recv, two_send, two_recv)
+
+    def own_gradient():
+        grad_block(0, lax.rem(stage, each), 0)
+        mine_g = g_buf.at[0]
+        for cols in tiles(width):
+            back = rows_dot(mine_g[:cut, :], table[:cut, cols]) + rows_dot(mine_g[cut:, :], table[cut:, cols])
+            parts[:, :, :, cols] = back.reshape(*parts.shape[:-1], TILE)
+            if cols.stop % half == 0:
+                red.begin(cols.start // half)
+
+    tops = []
     zero = jnp.zeros((8, pair), F32)
-    for b in range(pieces + 1):
-        def both(start, count, carry, b=b, top_b=top_b):
+    for now, done in ((0, None), (None, 0), (1, None), *((b, b - 1) for b in range(2, pieces)), (None, pieces - 1)):
+        label = None if done is None else jnp.concatenate([label_of(group_at(done, i)) for i in range(each)], axis=1)
+        top_b = None if done is None else tops[done]
+
+        def both(start, carry, now=now, done=done, top_b=top_b, label=label):
             best, total, hits = carry
-            if b < pieces:
-                best = jnp.maximum(best, logit_chunk(b, start, count))
-            if b > 0:
-                total, hits = exp_chunk(b - 1, start, count, top_b, total, hits)
+            if now is not None:
+                best = jnp.maximum(best, logit_chunk(now, start))
+            if done is not None:
+                total, hits = exp_chunk(done, start, label, top_b, total, hits)
             return best, total, hits
 
-        carry = (jnp.full((8, pair), -jnp.inf, F32), zero, zero)
-        best, total, hits = lax.fori_loop(0, rows // chunk, lambda c, carry: both(pl.multiple_of(c * chunk, 8), chunk, carry), carry)
-        if b > 0:
-            lse = top_b + jnp.log(jnp.sum(total, axis=0, keepdims=True))
-            hits = jnp.sum(hits, axis=0, keepdims=True)
-            for i in range(pair // group):
-                p = (b - 1) * (pair // group) + i
-                stat[0, p:p + 1, :] = lse[:, i * group:(i + 1) * group]
-                stat[1, p:p + 1, :] = hits[:, i * group:(i + 1) * group]
-                peak[p:p + 1, :] = top_b[:, i * group:(i + 1) * group]
-        if b < pieces:
-            top_b = jnp.max(best, axis=0, keepdims=True)
-        if b in (2, 3):
-            pl.when(top_plane)(functools.partial(next, ways[0][1]))
-        if b == pieces - 1:
-            pl.when(ways[1][0])(functools.partial(next, ways[1][1]))
-
-    def msg(d, kind):
-        return remote(stat.at[kind], shared.at[kind, tp], share_send.at[kind], share_recv.at[kind], {'tp': lax.rem(tp + d, size)})
-
-    for kind in BOTH:
-        for d in range(1, size):
-            msg(d, kind).start()
-        shared[kind, tp] = stat[kind]
-
-    def shares(kind):
-        ref = shared.at[kind, pl.ds(0, size - 1)]
-        return remote(ref, ref, share_send.at[kind], share_recv.at[kind], {'tp': plane.at(1, 0)})
-
-    shares(0).wait_recv()
-    every = shared[0]
-    most = jnp.max(every, axis=0)
-    log_norm = most + jnp.log(jnp.sum(jnp.exp(every - most[None]), axis=0))
-    scale_ref[:] = jnp.exp(peak[:] - log_norm)
-
-    def grad_block(p, slot):
-        e_ref = e_bufs[p // (pair // group)]
-        col = p % (pair // group) * group
-
-        def part(start, count):
-            e = e_ref[pl.ds(start, count), col:col + group]
-            hit = lab[p:p + 1, :] == start + lax.broadcasted_iota(jnp.int32, e.shape, 0)
-            g_buf[slot, pl.ds(start, count), :] = (e * scale_ref[p:p + 1, :] - jnp.where(hit, 1.0, 0.0)).astype(BF16)
-
-        @pl.loop(0, rows // chunk)
-        def _(c):
-            part(pl.multiple_of(c * chunk, 8), chunk)
-
-    def save(p):
-        slot = 1 + p % 2
-        return local(g_buf.at[slot], g_out.at[:, p * group:(p + 1) * group], loc_sem.at[2 + slot])
-
-    for p in range(stages):
-        pl.when(stage == p)(functools.partial(grad_block, p, 0))
-    cut = rows // group * group
-    red = Reduce(plane, parts, got_one, sum_one, got_two, one_send, one_recv, two_send, two_recv)
-    mine_g = g_buf.at[0]
-    half = width // 2
-    for cols in tiles(width):
-        back = contract(mine_g[:cut, :], table[:cut, cols], 0, 0) + contract(mine_g[cut:, :], table[cut:, cols], 0, 0)
-        parts[:, :, :, cols] = back.reshape(*parts.shape[:-1], TILE)
-        if cols.stop % half == 0:
-            red.begin(cols.start // half)
-    for p in range(stages):
-        if p >= 2:
-            save(p - 2).wait()
-        grad_block(p, 1 + p % 2)
-        save(p).start()
-    red.middle()
+        best, total, hits = chunks(both, (jnp.full((8, pair), -jnp.inf, F32), zero, zero))
+        if done is not None:
+            found = (top_b + jnp.log(jnp.sum(total, axis=0, keepdims=True)), jnp.sum(hits, axis=0, keepdims=True), top_b)
+            for i in range(each):
+                cols = slice(i * group, (i + 1) * group)
+                for kind in BOTH:
+                    stat[done, kind, i:i + 1, :] = found[kind][:, cols]
+                peak[done, i:i + 1, :] = found[2][:, cols]
+            shared[done, tp] = stat[done]
+        if now is None:
+            share(1 if done else 0)
+        else:
+            tops.append(jnp.max(best, axis=0, keepdims=True))
+        if now == 1:
+            normalise(0)
+            own_gradient()
+        if now == pieces - 1:
+            red.middle()
+
+    gradient(0)
+    gradient(1)
     sums = red.end()
 
     @pl.when(stage != target)
@@ -584,7 +634,8 @@
     inv_rms, normed = norm_of(own_x[:])
     mean = (jnp.sum(normed[:, :half] * sums[0], axis=-1, keepdims=True) + jnp.sum(normed[:, half:] * sums[1], axis=-1, keepdims=True)) / width
     for h in BOTH:
-        piece[:, h * half:(h + 1) * half] = (inv_rms * (sums[h] - normed[:, h * half:(h + 1) * half] * mean)).astype(BF16)
+        cols = slice(h * half, (h + 1) * half)
+        piece[:, cols] = (inv_rms * (sums[h] - normed[:, cols] * mean)).astype(BF16)
 
     def line(p):
         return remote(piece, g_top.at[p], line_send, line_recv, {'pp': target})
@@ -593,12 +644,10 @@
     def _():
         line(stage).start()
 
-    for here, steps in ways:
-        pl.when(here)(functools.partial(drain, steps))
-
-    save_x = local(x_all, x_out, loc_sem.at[2])
-    pl.when(upper)(save_x.start)
-
+    normalise(1)
+    for k in range(2, stages):
+        gradient(k)
+    loss_out[:] = sum(losses) / (stages * group)
     @pl.when(stage == target)
     def _():
         g_top[target] = piece[:]
@@ -606,11 +655,8 @@
         remote(got, got, line_send, line_recv, spread.mate).wait_recv()
 
     red.close()
-    pl.when(upper)(save_x.wait)
-    shares(1).wait_recv()
-    loss_out[:] = jnp.sum(log_norm - jnp.sum(shared[1], axis=0), keepdims=True) / (stages * group)
-    for kind in BOTH:
-        shares(kind).wait_send()
+    for k in BOTH:
+        shares(k).wait_send()
     save_n.wait()
     save(stages - 2).wait()
     save(stages - 1).wait()
@@ -626,7 +672,7 @@
         line(stage).wait_send()
 
 
-def backward_kernel(last, middle, chunk, g_top, hid_in, one_all, two_all, g_all, n_all, x_in, x_mid, w_one, w_two, de_buf, dx_all, grad_one, grad_two,
+def backward_kernel(last, chunk, g_top, hid_in, two_all, one_all, g_all, n_all, x_in, w_one, w_two, de_buf, dx_all, grad_one, grad_two,
                     ones, twos, slope_ref, g_buf, n_buf, x_all, w_one_buf, w_two_buf, dy_all, dy_buf, dx_buf, d_buf,
                     send_sem, recv_sem, spread_send, spread_recv, die_send, die_recv, hop_send, hop_recv, go_sem, ready_sem, g_sem, loc_sem):
     plane = Plane()
@@ -635,21 +681,26 @@
     blocks, cols, width = one_all.shape
     pairs = ((hid_in, slope_ref), (two_all, twos), (one_all, ones), (n_all, n_buf), (w_one, w_one_buf), (w_two, w_two_buf))
     loads = [local(src, dst, loc_sem.at[i]) for i, (src, dst) in enumerate(pairs)]
-    lower = stage < middle
-    load_x = [local(src, x_all, loc_sem.at[6]) for src in (x_in, x_mid)]
-
-    def load_rest(at):
-        for load in loads[3:] + [load_x[at]]:
+    lower = stage < SIDE
+    upper = stage >= SIDE
+    own = plane.tp
+    load_x = [local(*pair, loc_sem.at[6]) for pair in ((x_in, x_all), (x_in.at[own], x_all.at[own]))]
+
+    mid = upper & (stage < last - 1)
+
+    def start(some):
+        for load in some:
             load.start()
 
-    for load in loads[:3]:
-        load.start()
-    pl.when(lower)(functools.partial(load_rest, 0))
+    pl.when(upper)(functools.partial(start, loads[:3]))
+    pl.when(lower)(functools.partial(start, loads[3:4]))
+    own_load = load_x[1]
+    pl.when(mid)(own_load.start)
     spread = Spread(plane, 0, stages, dx_buf, dx_all, spread_send, spread_recv, die_send, die_recv)
     near = plane.near()
     for peer in near:
         signal(peer)
-    extra = spread.greet()
+    extra = spread.greet(0)
     before = {'pp': lax.rem(stage + last, stages)}
     pl.when(stage > 0)(functools.partial(signal, before))
     hop = remote(dx_buf, dy_buf, hop_send, hop_recv, before)
@@ -674,21 +725,35 @@
             def _():
                 fetch(c + 1).start()
 
+            for i, some in enumerate((loads[:2], loads[2:3], loads[4:] + load_x[:1])):
+                pl.when(lower & (c == i + 1))(functools.partial(start, some))
+
             fetch(c).wait()
-            de_buf[piece_at(c), :] = jnp.dot(g_buf[lax.rem(c, 2)], n_buf[:], preferred_element_type=F32)
+            de_buf[piece_at(c), :] = dot(g_buf[lax.rem(c, 2)], n_buf[:])
+
+    pl.semaphore_wait(pltpu.get_barrier_semaphore(), len(near) + extra + jnp.where(stage < last, 1, 0))
+
+    @pl.when(stage < last)
+    def _():
+        pl.semaphore_signal(ready_sem, inc=1, device_id={'pp': lax.rem(stage + 1, stages)}, device_id_type=MESH)
 
     pl.when(lower)(functools.partial(table, 0, pieces))
-    pl.semaphore_wait(pltpu.get_barrier_semaphore(), len(near) + extra + jnp.where(stage < last, 1, 0))
-
-    @pl.when(stage < last)
-    def _():
-        pl.semaphore_signal(ready_sem, inc=1, device_id={'pp': lax.rem(stage + 1, stages)}, device_id_type=MESH)
-
     loads[0].wait()
     for k in range(blocks):
         slope_ref[k] = gelu_slope(slope_ref[k])
     loads[1].wait()
 
+    def a_steps(begun=False):
+        return plane_gather(plane, [(x_all, 0, x_all.shape[1])], send_sem, recv_sem, base=2, begun=begun)
+
+    mid_steps = a_steps()
+
+    @pl.when(mid)
+    def _():
+        own_load.wait()
+        for _ in range(3):
+            next(mid_steps)
+
     @pl.when(stage == last)
     def _():
         dy_buf[:] = g_top[:]
@@ -707,12 +772,12 @@
 
     grad_y = dy_buf[:]
     for k in range(blocks):
-        grad_gate = jnp.dot(grad_y, twos[k], preferred_element_type=F32)
+        grad_gate = dot(grad_y, twos[k])
         d_buf[:, k * cols:(k + 1) * cols] = (slope_ref[k] * grad_gate).astype(BF16)
     loads[2].wait()
     grad_hidden = d_buf[:]
     for tile in tiles(width):
-        back = jnp.dot(grad_hidden, ones[:, :, tile].reshape(blocks * cols, TILE), preferred_element_type=F32)
+        back = dot(grad_hidden, ones[:, :, tile].reshape(blocks * cols, TILE))
         dx_buf[:, tile] = (dy_buf[:, tile].astype(F32) + back).astype(BF16)
 
     @pl.when(stage > 0)
@@ -721,10 +786,12 @@
         hop.start()
 
     pl.when(stage == 0)(spread.send)
-    pl.when(jnp.logical_not(lower))(functools.partial(load_rest, 1))
+    pl.when(upper)(functools.partial(start, loads[3:]))
+    pl.when(upper & jnp.logical_not(mid))(own_load.start)
     for load in loads[4:]:
         load.wait()
-    load_x[0].wait()
+    pl.when(lower)(load_x[0].wait)
+    pl.when(upper & jnp.logical_not(mid))(own_load.wait)
 
     grad_one[:] = jnp.zeros_like(grad_one)
     grad_two[:] = jnp.zeros_like(grad_two)
@@ -737,11 +804,11 @@
             part = pl.ds(c * step, step)
             x_act = x_all[part].reshape(step * x_all.shape[1], width)
             grad_y = dy_all[part].reshape(step * x_all.shape[1], width)
-            hidden = jnp.dot(x_act, w_one_buf[:], preferred_element_type=F32)
-            grad_gate = contract(grad_y, w_two_buf[:], 1, 1)
+            hidden = dot(x_act, w_one_buf[:])
+            grad_gate = cols_dot(grad_y, w_two_buf[:])
             grad_hidden = (gelu_slope(hidden) * grad_gate).astype(BF16)
-            grad_one[:] += contract(x_act, grad_hidden, 0, 0)
-            grad_two[:] += contract(gelu(hidden).astype(BF16), grad_y, 0, 0)
+            grad_one[:] += rows_dot(x_act, grad_hidden)
+            grad_two[:] += rows_dot(gelu(hidden).astype(BF16), grad_y)
 
     def dx_steps():
         return plane_gather(plane, [part], send_sem, recv_sem, spread.on_block)
@@ -758,28 +825,32 @@
         def _():
             pl.semaphore_wait(go_sem, 1)
 
+    @pl.when(stage > 1)
+    def _():
         next(dy_steps(False))
 
-    @pl.when(jnp.logical_not(lower))
-    def _():
-        steps = dy_steps(True)
-        for lo in range(0, pieces, 3):
-            next(steps)
-            table(lo, min(lo + 3, pieces))
-            next(steps)
-        drain(steps)
-
-    planes = [(stage <= 1, 'dxddxdxdxdx', 'xx'), ((stage > 1) & lower, 'dddxdxdxdx', 'xxx')]
+    @pl.when(upper & jnp.logical_not(mid))
+    def _():
+        next(a_steps())
+
+    planes = [(stage <= 1, None, 'dxddxdxdxdx', 'xx'), ((stage > 1) & lower, None, 'dddxdxdxdx', 'xxx'),
+              (mid, mid_steps, 'dtdadatdaxdaxdx', 'xxx'), (upper & jnp.logical_not(mid), a_steps(True), 'datdadatdaxdaxdax', 'xxx')]
     runs = []
-    for here, order, rest in planes:
-        steps = {'d': dy_steps(True), 'x': dx_steps()}
+    for here, more, order, rest in planes:
+        steps = {'d': dy_steps(True), 'x': dx_steps(), 'a': more}
 
         def arrived(order=order, steps=steps):
+            part = -(-pieces // 2)
             for i, kind in enumerate(order):
+                if kind == 't':
+                    lo = order[:i].count('t') * part
+                    table(lo, min(lo + part, pieces))
+                    continue
                 if kind == 'x' and 'x' not in order[:i]:
                     pl.when(stage > 0)(spread.arrive)
                 next(steps[kind])
             drain(steps['d'])
+            drain(steps['a'] or ())
 
         def onward(rest=rest, steps=steps):
             for kind in rest:
@@ -794,11 +865,6 @@
     weights(2, SIDE)
     for here, _, finish in runs:
         pl.when(here)(finish)
-
-    @pl.when(jnp.logical_not(lower))
-    def _():
-        spread.arrive()
-        drain(dx_steps())
 
     spread.finish()
     spread.close()
@@ -865,10 +931,12 @@
         def reduce_scratch(dtype):
             return [VM((SIDE, SIDE, unit, width), dtype), VM((6, SIDE, unit, half), dtype), VM((2, SIDE, unit, half), dtype), VM((6, unit, half), dtype), VM((unit, width), BF16)]
 
-        reduce_sems = [DMA, DMA((2,)), DMA, DMA((2,)), DMA, DMA]
+        duo = DMA((2,))
+        reduce_sems = [DMA, duo, DMA, duo, DMA, DMA]
         many = shape((tp_size, block, width), BF16)
         many_buf = VM((tp_size, block, width), BF16)
         two_sums = 2 * SLOTS
+        gather_sems = [DMA((3,)), DMA((3 * two_sums,))]
 
         y_act, order, hidden, one_t, two_t, x_all = pl.pallas_call(
             functools.partial(forward_kernel, last),
@@ -879,35 +947,35 @@
                             VM((vocab_rows, width), BF16), VM((vocab_rows, group), BF16), *reduce_scratch(BF16),
                             VM((block, width), BF16), VM((block, width), BF16), VM((block, tp_size * cols), BF16), VM((tp_size, block, cols), F32), many_buf, VM((1, group), jnp.int32),
                             VM((num_tokens // 128, 128), jnp.int32), VM((2, num_tokens), jnp.int32),
-                            DMA((3,)), DMA((3 * two_sums,)), *reduce_sems, DMA, DMA, DMA((7,))],
+                            *gather_sems, *reduce_sems, DMA, DMA, pltpu.SemaphoreType.REGULAR, DMA((7,))],
             compiler_params=params(1, 58), name='forward_chain',
         )(tokens, emb_table, w_one, w_two)
 
         spread_sems = [DMA, DMA, DMA, DMA]
-        middle = pp_size // 2
-        loss, g_top, g_all, n_all, x_mid = pl.pallas_call(
-            functools.partial(head_kernel, last, pp_size, middle, chunk),
-            out_shape=(shape((1, 1), F32), shape((pp_size, unit, width), BF16), shape((vocab_rows, num_tokens), BF16), shape((num_tokens, width), BF16), many),
-            in_specs=[anywhere(), vmem(), vmem(), anywhere()],
-            out_specs=[vmem()] * 2 + [anywhere()] * 3,
+        by_pair = (num_tokens // pair, pair // group, group)
+        loss, g_top, g_all, n_all = pl.pallas_call(
+            functools.partial(head_kernel, last, pp_size, chunk),
+            out_shape=(shape((1, 1), F32), shape((pp_size, unit, width), BF16), shape((vocab_rows, num_tokens), BF16), shape((num_tokens, width), BF16)),
+            in_specs=[anywhere(), vmem(), vmem()],
+            out_specs=[vmem()] * 2 + [anywhere()] * 2,
             scratch_shapes=[VM((vocab_rows, width), BF16), many_buf, VM((unit, width), BF16), VM((block, width), BF16), VM((num_tokens, width), BF16),
-                            many_buf, VM((pp_size, group), jnp.int32), VM((3, vocab_rows, group), BF16),
-                            VM((pp_size, group), F32), VM((2, pp_size, group), F32), VM((2, tp_size, pp_size, group), F32), VM((pp_size, group), F32), *reduce_scratch(F32),
-                            DMA((2,)), DMA((2 * two_sums,)), DMA((2,)), DMA((2,)), DMA, DMA, *spread_sems, *reduce_sems, DMA((5,)),
+                            VM((pp_size, group), jnp.int32), VM((3, vocab_rows, group), BF16),
+                            VM(by_pair, F32), VM((by_pair[0], 2, *by_pair[1:]), F32), VM((by_pair[0], tp_size, 2, *by_pair[1:]), F32), VM(by_pair, F32), *reduce_scratch(F32),
+                            *gather_sems, duo, duo, DMA, DMA, *spread_sems, *reduce_sems, DMA((5,)),
                             *[VM((vocab_rows, pair), F32) for _ in range(num_tokens // pair)]],
             compiler_params=params(2, 60), name='head',
-        )(emb_table, y_act, labels, x_all)
+        )(emb_table, y_act, labels)
 
         de_head, dx_first, grad_one, grad_two = pl.pallas_call(
-            functools.partial(backward_kernel, last, middle, step),
+            functools.partial(backward_kernel, last, step),
             out_shape=(VM((vocab_rows, width), F32), many_buf, VM((width, cols), F32), VM((cols, width), F32)),
-            in_specs=[vmem()] + [anywhere()] * 9, out_specs=[vmem()] * 4,
+            in_specs=[vmem()] + [anywhere()] * 8, out_specs=[vmem()] * 4,
             scratch_shapes=[VM((tp_size, cols, width), BF16), VM((tp_size, width, cols), BF16), VM((tp_size, block, cols), F32), VM((2, step, num_tokens), BF16), VM((num_tokens, width), BF16),
                             many_buf, VM((width, cols), BF16), VM((cols, width), BF16), many_buf,
                             VM((block, width), BF16), VM((block, width), BF16), VM((block, tp_size * cols), BF16),
-                            DMA((3,)), DMA((3 * two_sums,)), *spread_sems, DMA, DMA, pltpu.SemaphoreType.REGULAR, pltpu.SemaphoreType.REGULAR, DMA((2,)), DMA((7,))],
-            compiler_params=params(3, 44), name='backward_chain',
-        )(g_top.reshape(block, width), hidden, one_t, two_t, g_all, n_all, x_all, x_mid, w_one, w_two)
+                            *gather_sems, *spread_sems, DMA, DMA, pltpu.SemaphoreType.REGULAR, pltpu.SemaphoreType.REGULAR, duo, DMA((7,))],
+            compiler_params=params(3, 45), name='backward_chain',
+        )(g_top.reshape(block, width), hidden, two_t, one_t, g_all, n_all, x_all, w_one, w_two)
 
         smem = pl.BlockSpec(memory_space=pltpu.SMEM)
         _, grad_table, grad_one, grad_two = pl.pallas_call(

time: 314 us -> 295 us (0.939)
  Pallas kernels: 311 us -> 292 us
    pallas_call x2, Pallas kernels: 170 us -> 153 us  [the longest x1 83.6 us: device_fn(): pl.pallas_call(functools.partial(backward_kernel, last, step), out_shape=...]
where the time goes in v1:
time: 295 us
  Pallas kernels  292 us (99%)
    pallas_call x1, Pallas kernels, device_fn(): pl.pallas_call(functools.partial(forward_kernel, last), out_shape=(shape(...  131 us
    pallas_call x1, Pallas kernels, device_fn(): pl.pallas_call(functools.partial(backward_kernel, last, step), out_shape=...  83.6 us
    pallas_call x1, Pallas kernels, device_fn(): pl.pallas_call(functools.partial(head_kernel, last, pp_size, chunk), out_...  69.9 us
    pallas_call x1, Pallas kernels, device_fn(): pl.pallas_call(functools.partial(add_kernel, 12), out_shape=(VM((vocab_ro...  7.92 us

profile of v1, /device:TPU:1, one launch (start us, length us, event | category | flops | bytes accessed | tf_op | source)
XLA Modules:
  0.0 294.6 jit_solution(17072658642082141324)
XLA Ops:
  0.6 130.8 %forward_chain.1 = (bf16[128,1024]{1,0:T(8,128)(2,1)}, s32[3,2048]{1,0:T(4,128)}, f32[16,128,256]{2,1,0:T(8,128)}, bf16[16,256,1024]{2,1,0:T(8,128)(2,1)}, bf16[...) custom-call(s32[32,64]{1,0:T(8,128)} %tokens.1, bf16[3144,1024]{1,0:T(8,128)(2,1)} %emb.3, ...), custom_call_target="tpu_custom_call" | custom-call | tf_op jit(solution)/shard_map/forward_chain/pallas_call | solution.py:941
  131.5 69.9 %head.1 = (f32[1,1]{1,0:T(1,128)}, bf16[8,16,1024]{2,1,0:T(8,128)(2,1)}, bf16[3144,2048]{1,0:T(8,128)(2,1)}, bf16[2048,1024]{1,0:T(8,128)(2,1)}) custom-call(bf16[3144,1024]{1,0:T(8,128)(2,1)} %emb.3, bf16[128,1024]{1,0:T(8,128)(2,1)} %get-tuple-element.21.y_ref, s32[32,64]{1,0:T(8,128)} %labels.1), custom_call_target="tpu_custom_call" | custom-call | tf_op jit(solution)/shard_map/head/pallas_call | solution.py:956
  201.3 0.0 copy-start
  201.3 83.6 %backward_chain.1 = (f32[3144,1024]{1,0:T(8,128)S(1)}, bf16[16,128,1024]{2,1,0:T(8,128)(2,1)S(1)}, f32[1024,256]{1,0:T(8,128)S(1)}, f32[256,1024]{1,0:T(8,128)S(1)}) custom-call(bf16[128,1024]{1,0:T(8,128)(2,1)} %bitcast.12, f32[16,128,256]{2,1,0:T(8,128)} %get-tuple-element.25.hid_in, bf16[16,1024,256]{2,1,0:T(8,128)(2,1)} %get-tuple-element.26.two_all, ...), custom_call_target="tpu_custom_call" | custom-call | tf_op jit(solution)/shard_map/backward_chain/pallas_call | solution.py:969
  284.9 0.0 copy-done
  284.9 7.9 %add_rows.1 = (f32[3144,1024]{1,0:T(8,128)S(1)}, f32[3144,1024]{1,0:T(8,128)}, f32[1024,256]{1,0:T(8,128)}, f32[256,1024]{1,0:T(8,128)}) custom-call(s32[3,2048]{1,0:T(4,128)S(1)} %copy-done, bf16[2048,1024]{1,0:T(8,128)(2,1)S(1)} %bitcast.7, f32[3144,1024]{1,0:T(8,128)S(1)} %get-tuple-element.32.de_ref, ...), custom_call_target="tpu_custom_call", output_to_operand_aliasing={{0}: (2, {})} | custom-call | tf_op jit(solution)/shard_map/add_rows/pallas_call | solution.py:981
Async XLA Ops:
  201.3 83.6 %copy-start = (s32[3,2048]{1,0:T(4,128)S(1)}, s32[3,2048]{1,0:T(4,128)}, u32[]{:S(2)}) copy-start(s32[3,2048]{1,0:T(4,128)} %get-tuple-element.23.order) | copy-start | bytes 73732

commit v2 on v1

--- a/solution.py
+++ b/solution.py
@@ -252,9 +252,71 @@
     out[2:, :] = jnp.broadcast_to(total, (1, count)).astype(jnp.int32)
 
 
-def forward_kernel(last, tokens, emb, w_one, w_two, y_out, order_out, hid_out, one_out, two_out, x_out, ones, twos, one_t, two_t, table, hot, parts,
-                   got_one, sum_one, got_two, piece, x_buf, y_buf, a_buf, hid_ref, x_all, ids, flat, slot,
-                   send_sem, recv_sem, one_send, one_recv, two_send, two_recv, line_send, line_recv, hop_send, hop_recv, lead_sem, loc_sem):
+def norm_of(x):
+    wide = x.astype(F32)
+    inv_rms = lax.rsqrt(jnp.mean(wide * wide, axis=-1, keepdims=True) + NORM_EPS)
+    return inv_rms, wide * inv_rms
+
+
+class Spread:
+    def __init__(self, plane, source, stages, src, out, line_send, line_recv, die_send, die_recv):
+        self.plane, self.source, self.stages, self.src, self.out = plane, source, stages, src, out
+        self.line_send, self.line_recv, self.die_send, self.die_recv = line_send, line_recv, die_send, die_recv
+        self.stage = lax.axis_index('pp')
+        self.core = lax.rem(self.stage, 2)
+        self.mate = {'pp': self.stage + 1 - 2 * self.core}
+        self.rows = out.shape[1] // 2
+        self.lo = pl.multiple_of(self.core * self.rows, self.rows)
+        self.others = [p for p in range(stages) if p != source]
+
+    def greet(self):
+        source = self.stage == self.source
+        twin = self.stage == self.source ^ 1
+        pl.when(source)(functools.partial(signal, {'pp': self.source ^ 1}))
+        pl.when(jnp.logical_not(source))(functools.partial(signal, {'pp': self.source}))
+        pl.when(jnp.logical_not(source | twin))(functools.partial(signal, self.mate))
+        return jnp.where(source, len(self.others), 1)
+
+    def line(self, p):
+        part = pl.ds((p % 2) * self.rows, self.rows)
+        return remote(self.src.at[part], self.out.at[self.plane.tp, part], self.line_send, self.line_recv, {'pp': p})
+
+    def send(self):
+        for p in self.others:
+            self.line(p).start()
+        part = pl.ds(self.lo, self.rows)
+        self.out[self.plane.tp, part] = self.src[part]
+
+    def arrive(self):
+        mine = self.out.at[self.plane.tp, pl.ds(self.lo, self.rows)]
+        remote(mine, mine, self.line_recv, self.line_recv, self.mate).wait_recv()
+
+    def on_block(self, a, half, j, k):
+        if a == 0:
+            size = self.rows // 2
+            ref = self.out.at[self.plane.blk(half, HOPS[j], HOPS[k]), pl.ds(self.lo + half * size, size)]
+            remote(ref, ref, self.die_send, self.die_recv, self.mate).start()
+
+    def half(self, lo):
+        ref = self.out.at[:, pl.ds(lo, self.rows)]
+        return remote(ref, ref, self.die_send, self.die_recv, self.mate)
+
+    def finish(self):
+        self.half(pl.multiple_of((1 - self.core) * self.rows, self.rows)).wait_recv()
+
+    def close(self):
+        self.half(self.lo).wait_send()
+
+        @pl.when(self.stage == self.source)
+        def _():
+            sent = self.out.at[pl.ds(0, len(self.others)), pl.ds(self.lo, self.rows)]
+            remote(sent, sent, self.line_send, self.line_recv, self.mate).wait_send()
+
+
+def forward_kernel(last, tokens, emb, w_one, w_two, top, own_x, table, order_out, hid_out, one_out, two_out, x_out, ones, twos, one_t, two_t, hot, parts,
+                   got_one, sum_one, got_two, piece, x_buf, y_buf, n_src, a_buf, hid_ref, x_all, ids, flat, slot,
+                   send_sem, recv_sem, one_send, one_recv, two_send, two_recv, line_send, line_recv, own_send, own_recv, spread_send, spread_recv, die_send, die_recv,
+                   hop_send, hop_recv, lead_sem, loc_sem):
     plane = Plane()
     stage = lax.axis_index('pp')
     tp = plane.tp
@@ -363,7 +425,6 @@
         y_buf[:, tile] = (x_buf[:, tile].astype(F32) + branch).astype(BF16)
 
     pl.when(stage < last)(hop.start)
-    y_out[:] = y_buf[:]
     x_all[tp] = x_buf[:]
 
     @pl.when(stage < SIDE)
@@ -380,6 +441,31 @@
     own_save = local(x_all.at[tp], x_out.at[tp], loc_sem.at[6])
     pl.when(stage < SIDE)(save_x.start)
     pl.when(stage >= SIDE)(own_save.start)
+
+    spread = Spread(plane, last, stages, n_src, top, spread_send, spread_recv, die_send, die_recv)
+
+    def own(p):
+        return remote(y_buf.at[pl.ds(p * unit, unit)], own_x, own_send, own_recv, {'pp': p})
+
+    @pl.when(stage == last)
+    def _():
+        n_src[:] = norm_of(y_buf[:])[1].astype(BF16)
+        spread.send()
+        for p in spread.others:
+            own(p).start()
+        own_x[:] = y_buf[last * unit:]
+
+    pl.when(stage < last)(spread.arrive)
+    drain(plane_gather(plane, [(top, spread.lo, spread.rows)], send_sem, recv_sem, spread.on_block, base=3))
+    spread.finish()
+    pl.when(stage < last)(own(last).wait_recv)
+    spread.close()
+
+    @pl.when(stage == last)
+    def _():
+        sent = y_buf.at[pl.ds(0, last * unit)]
+        remote(sent, sent, own_send, own_recv, spread.mate).wait_send()
+
     red.close()
 
     @pl.when(stage != 0)
@@ -393,113 +479,29 @@
     pl.when(stage >= SIDE)(own_save.wait)
 
 
-def norm_of(x):
-    wide = x.astype(F32)
-    inv_rms = lax.rsqrt(jnp.mean(wide * wide, axis=-1, keepdims=True) + NORM_EPS)
-    return inv_rms, wide * inv_rms
-
-
-class Spread:
-    def __init__(self, plane, source, stages, src, out, line_send, line_recv, die_send, die_recv):
-        self.plane, self.source, self.stages, self.src, self.out = plane, source, stages, src, out
-        self.line_send, self.line_recv, self.die_send, self.die_recv = line_send, line_recv, die_send, die_recv
-        self.stage = lax.axis_index('pp')
-        self.core = lax.rem(self.stage, 2)
-        self.mate = {'pp': self.stage + 1 - 2 * self.core}
-        self.rows = out.shape[1] // 2
-        self.lo = pl.multiple_of(self.core * self.rows, self.rows)
-        self.others = [p for p in range(stages) if p != source]
-
-    def greet(self, back):
-        source = self.stage == self.source
-        twin = self.stage == self.source ^ 1
-
-        @pl.when(source)
-        def _():
-            for p in self.others if back else [self.source ^ 1]:
-                signal({'pp': p})
-
-        @pl.when(jnp.logical_not(source))
-        def _():
-            signal({'pp': self.source})
-
-        pl.when(jnp.logical_not(source | twin))(functools.partial(signal, self.mate))
-        return jnp.where(source, len(self.others), jnp.where(twin, 1, 1 + back))
-
-    def line(self, p):
-        part = pl.ds((p % 2) * self.rows, self.rows)
-        return remote(self.src.at[part], self.out.at[self.plane.tp, part], self.line_send, self.line_recv, {'pp': p})
-
-    def send(self):
-        for p in self.others:
-            self.line(p).start()
-        part = pl.ds(self.lo, self.rows)
-        self.out[self.plane.tp, part] = self.src[part]
-
-    def arrive(self):
-        mine = self.out.at[self.plane.tp, pl.ds(self.lo, self.rows)]
-        remote(mine, mine, self.line_recv, self.line_recv, self.mate).wait_recv()
-
-    def on_block(self, a, half, j, k):
-        if a == 0:
-            size = self.rows // 2
-            ref = self.out.at[self.plane.blk(half, HOPS[j], HOPS[k]), pl.ds(self.lo + half * size, size)]
-            remote(ref, ref, self.die_send, self.die_recv, self.mate).start()
-
-    def half(self, lo):
-        ref = self.out.at[:, pl.ds(lo, self.rows)]
-        return remote(ref, ref, self.die_send, self.die_recv, self.mate)
-
-    def finish(self):
-        self.half(pl.multiple_of((1 - self.core) * self.rows, self.rows)).wait_recv()
-
-    def close(self):
-        self.half(self.lo).wait_send()
-
-        @pl.when(self.stage == self.source)
-        def _():
-            sent = self.out.at[pl.ds(0, len(self.others)), pl.ds(self.lo, self.rows)]
-            remote(sent, sent, self.line_send, self.line_recv, self.mate).wait_send()
-
-
-def head_kernel(target, stages, chunk, emb, y_ref, labels, loss_out, g_top, g_out, n_out,
-                table, top, own_x, n_src, n_buf, lab, g_buf, peak, stat, shared, scale_ref, parts, got_one, sum_one, got_two, piece,
-                send_sem, recv_sem, share_send, share_recv, own_send, own_recv, spread_send, spread_recv, die_send, die_recv,
-                one_send, one_recv, two_send, two_recv, line_send, line_recv, loc_sem, *e_bufs):
+def head_kernel(target, stages, chunk, table, top, own_x, labels, loss_out, g_top, g_out, n_out,
+                n_buf, lab, g_buf, peak, stat, shared, scale_ref, parts, got_one, sum_one, got_two, piece,
+                share_send, share_recv, one_send, one_recv, two_send, two_recv, line_send, line_recv, loc_sem, *e_bufs):
     plane = Plane()
     stage = lax.axis_index('pp')
     tp = plane.tp
     size = shared.shape[1]
     others = [p for p in range(stages) if p != target]
-    load = local(emb, table, loc_sem.at[0])
-    load.start()
-    spread = Spread(plane, target, stages, n_src, top, spread_send, spread_recv, die_send, die_recv)
+    each, group = peak.shape[1:]
+    unit = group // size
     for d in range(1, size):
         signal({'tp': lax.rem(tp + d, size)})
-    extra = spread.greet(1)
-    n_src[:] = norm_of(y_ref[:])[1].astype(BF16)
-    each, group = peak.shape[1:]
-    unit = group // size
-    pl.semaphore_wait(pltpu.get_barrier_semaphore(), size - 1 + extra)
-
-    def own(p):
-        return remote(y_ref.at[pl.ds(p * unit, unit)], own_x, own_send, own_recv, {'pp': p})
 
     @pl.when(stage == target)
     def _():
-        spread.send()
         for p in others:
-            own(p).start()
-        own_x[:] = y_ref[target * unit:(target + 1) * unit]
-
-    pl.when(stage != target)(spread.arrive)
-    drain(plane_gather(plane, [(top, spread.lo, spread.rows)], send_sem, recv_sem, spread.on_block))
-    spread.finish()
+            signal({'pp': p})
+
+    pl.when(stage != target)(functools.partial(signal, {'pp': target}))
     for p in range(stages):
         n_buf[p * group:(p + 1) * group] = top[:, p * unit:(p + 1) * unit, :].reshape(group, top.shape[2])
     save_n = local(n_buf, n_out, loc_sem.at[1])
     save_n.start()
-    load.wait()
 
     rows, width = table.shape
     flatten(labels, lab)
@@ -613,6 +615,8 @@
                     stat[done, kind, i:i + 1, :] = found[kind][:, cols]
                 peak[done, i:i + 1, :] = found[2][:, cols]
             shared[done, tp] = stat[done]
+        if done == 0:
+            pl.semaphore_wait(pltpu.get_barrier_semaphore(), size - 1 + jnp.where(stage == target, len(others), 1))
         if now is None:
             share(1 if done else 0)
         else:
@@ -627,10 +631,6 @@
     gradient(1)
     sums = red.end()
 
-    @pl.when(stage != target)
-    def _():
-        remote(own_x, own_x, own_recv, own_recv, spread.mate).wait_recv()
-
     inv_rms, normed = norm_of(own_x[:])
     mean = (jnp.sum(normed[:, :half] * sums[0], axis=-1, keepdims=True) + jnp.sum(normed[:, half:] * sums[1], axis=-1, keepdims=True)) / width
     for h in BOTH:
@@ -652,7 +652,7 @@
     def _():
         g_top[target] = piece[:]
         got = g_top.at[pl.ds(0, len(others))]
-        remote(got, got, line_send, line_recv, spread.mate).wait_recv()
+        remote(got, got, line_send, line_recv, {'pp': 0}).wait_recv()
 
     red.close()
     for k in BOTH:
@@ -660,13 +660,6 @@
     save_n.wait()
     save(stages - 2).wait()
     save(stages - 1).wait()
-    spread.close()
-
-    @pl.when(stage == target)
-    def _():
-        sent = y_ref.at[pl.ds(0, len(others) * unit)]
-        remote(sent, sent, own_send, own_recv, spread.mate).wait_send()
-
     @pl.when(stage != target)
     def _():
         line(stage).wait_send()
@@ -700,7 +693,7 @@
     near = plane.near()
     for peer in near:
         signal(peer)
-    extra = spread.greet(0)
+    extra = spread.greet()
     before = {'pp': lax.rem(stage + last, stages)}
     pl.when(stage > 0)(functools.partial(signal, before))
     hop = remote(dx_buf, dy_buf, hop_send, hop_recv, before)
@@ -936,35 +929,34 @@
         many = shape((tp_size, block, width), BF16)
         many_buf = VM((tp_size, block, width), BF16)
         two_sums = 2 * SLOTS
-        gather_sems = [DMA((3,)), DMA((3 * two_sums,))]
-
-        y_act, order, hidden, one_t, two_t, x_all = pl.pallas_call(
+        gather_sems = [DMA((4,)), DMA((4 * two_sums,))]
+        spread_sems = [DMA, DMA, DMA, DMA]
+
+        top, own_x, table, order, hidden, one_t, two_t, x_all = pl.pallas_call(
             functools.partial(forward_kernel, last),
-            out_shape=(shape((block, width), BF16), shape((3, num_tokens), jnp.int32), shape((tp_size, block, cols), F32), shape((tp_size, cols, width), BF16), shape((tp_size, width, cols), BF16), many),
+            out_shape=(many_buf, VM((unit, width), BF16), VM((vocab_rows, width), BF16), shape((3, num_tokens), jnp.int32), shape((tp_size, block, cols), F32), shape((tp_size, cols, width), BF16), shape((tp_size, width, cols), BF16), many),
             in_specs=[vmem()] + [anywhere()] * 3,
-            out_specs=[vmem()] * 2 + [anywhere()] * 4,
+            out_specs=[vmem()] * 4 + [anywhere()] * 4,
             scratch_shapes=[VM((tp_size, width, cols), BF16), VM((tp_size, cols, width), BF16), VM((tp_size, cols, width), BF16), VM((tp_size, width, cols), BF16),
-                            VM((vocab_rows, width), BF16), VM((vocab_rows, group), BF16), *reduce_scratch(BF16),
-                            VM((block, width), BF16), VM((block, width), BF16), VM((block, tp_size * cols), BF16), VM((tp_size, block, cols), F32), many_buf, VM((1, group), jnp.int32),
+                            VM((vocab_rows, group), BF16), *reduce_scratch(BF16),
+                            VM((block, width), BF16), VM((block, width), BF16), VM((block, width), BF16), VM((block, tp_size * cols), BF16), VM((tp_size, block, cols), F32), many_buf, VM((1, group), jnp.int32),
                             VM((num_tokens // 128, 128), jnp.int32), VM((2, num_tokens), jnp.int32),
-                            *gather_sems, *reduce_sems, DMA, DMA, pltpu.SemaphoreType.REGULAR, DMA((7,))],
-            compiler_params=params(1, 58), name='forward_chain',
+                            *gather_sems, *reduce_sems, DMA, DMA, *spread_sems, DMA, DMA, pltpu.SemaphoreType.REGULAR, DMA((7,))],
+            compiler_params=params(1, 49), name='forward_chain',
         )(tokens, emb_table, w_one, w_two)
 
-        spread_sems = [DMA, DMA, DMA, DMA]
         by_pair = (num_tokens // pair, pair // group, group)
         loss, g_top, g_all, n_all = pl.pallas_call(
             functools.partial(head_kernel, last, pp_size, chunk),
-            out_shape=(shape((1, 1), F32), shape((pp_size, unit, width), BF16), shape((vocab_rows, num_tokens), BF16), shape((num_tokens, width), BF16)),
-            in_specs=[anywhere(), vmem(), vmem()],
+            out_shape=(shape((1, 1), F32), pltpu.HBM((pp_size, unit, width), BF16), shape((vocab_rows, num_tokens), BF16), shape((num_tokens, width), BF16)),
+            in_specs=[vmem()] * 4,
             out_specs=[vmem()] * 2 + [anywhere()] * 2,
-            scratch_shapes=[VM((vocab_rows, width), BF16), many_buf, VM((unit, width), BF16), VM((block, width), BF16), VM((num_tokens, width), BF16),
-                            VM((pp_size, group), jnp.int32), VM((3, vocab_rows, group), BF16),
+            scratch_shapes=[VM((num_tokens, width), BF16), VM((pp_size, group), jnp.int32), VM((3, vocab_rows, group), BF16),
                             VM(by_pair, F32), VM((by_pair[0], 2, *by_pair[1:]), F32), VM((by_pair[0], tp_size, 2, *by_pair[1:]), F32), VM(by_pair, F32), *reduce_scratch(F32),
-                            *gather_sems, duo, duo, DMA, DMA, *spread_sems, *reduce_sems, DMA((5,)),
+                            duo, duo, *reduce_sems, DMA((5,)),
                             *[VM((vocab_rows, pair), F32) for _ in range(num_tokens // pair)]],
-            compiler_params=params(2, 60), name='head',
-        )(emb_table, y_act, labels)
+            compiler_params=params(2, 49), name='head',
+        )(*[pltpu.with_memory_space_constraint(array, pltpu.VMEM) for array in (table, top, own_x)], labels)
 
         de_head, dx_first, grad_one, grad_two = pl.pallas_call(
             functools.partial(backward_kernel, last, step),

time: 295 us -> 290 us (0.983)
  Pallas kernels: 292 us -> 287 us
    pallas_call x1, Pallas kernels: 69.9 us -> 37 us  [device_fn(): pl.pallas_call(functools.partial(head_kernel, last, pp_size, chunk), out_...]
    pallas_call x1, Pallas kernels: 131 us -> 158 us  [device_fn(): pl.pallas_call(functools.partial(forward_kernel, last), out_shape=(many_b...]
where the time goes in v2:
time: 290 us; the launch traced here: 289 us
  Pallas kernels  287 us (99%)
    pallas_call x1, Pallas kernels, device_fn(): pl.pallas_call(functools.partial(forward_kernel, last), out_shape=(many_b...  158 us
    pallas_call x1, Pallas kernels, device_fn(): pl.pallas_call(functools.partial(backward_kernel, last, step), out_shape=...  83.7 us
    pallas_call x1, Pallas kernels, device_fn(): pl.pallas_call(functools.partial(head_kernel, last, pp_size, chunk), out_...  37 us
    pallas_call x1, Pallas kernels, device_fn(): pl.pallas_call(functools.partial(add_kernel, 12), out_shape=(VM((vocab_ro...  7.91 us

profile of v2, /device:TPU:1, one launch (start us, length us, event | category | flops | bytes accessed | tf_op | source)
XLA Modules:
  0.0 289.5 jit_solution(15675550083725576941)
XLA Ops:
  0.6 158.5 %forward_chain.1 = (bf16[16,128,1024]{2,1,0:T(8,128)(2,1)S(1)}, bf16[16,1024]{1,0:T(8,128)(2,1)S(1)}, bf16[3144,1024]{1,0:T(8,128)(2,1)S(1)}, s32[3,2048]{1,0:T(...) custom-call(s32[32,64]{1,0:T(8,128)} %tokens.1, ...), custom_call_target="tpu_custom_call" | custom-call | tf_op jit(solution)/shard_map/forward_chain/pallas_call | solution.py:935
  159.1 37.0 %head.1 = (f32[1,1]{1,0:T(1,128)}, bf16[8,16,1024]{2,1,0:T(8,128)(2,1)}, bf16[3144,2048]{1,0:T(8,128)(2,1)}, bf16[2048,1024]{1,0:T(8,128)(2,1)}) custom-call(bf16[3144,1024]{1,0:T(8,128)(2,1)S(1)} %get-tuple-element.23.table, bf16[16,128,1024]{2,1,0:T(8,128)(2,1)S(1)} %get-tuple-element.24.top, bf16[16,1024]{1,0:T(8,128)(2,1)S(1)} %get-tuple-element.25.own_x, ...), custom_call_target="tpu_custom_call" | custom-call | tf_op jit(solution)/shard_map/head/pallas_call | solution.py:949
  196.1 0.0 copy-start
  196.1 83.7 %backward_chain.1 = (f32[3144,1024]{1,0:T(8,128)S(1)}, bf16[16,128,1024]{2,1,0:T(8,128)(2,1)S(1)}, f32[1024,256]{1,0:T(8,128)S(1)}, f32[256,1024]{1,0:T(8,128)S(1)}) custom-call(bf16[128,1024]{1,0:T(8,128)(2,1)} %bitcast.12, f32[16,128,256]{2,1,0:T(8,128)} %get-tuple-element.29.hid_in, bf16[16,1024,256]{2,1,0:T(8,128)(2,1)} %get-tuple-element.30.two_all, ...), custom_call_target="tpu_custom_call" | custom-call | tf_op jit(solution)/shard_map/backward_chain/pallas_call | solution.py:961
  279.8 0.0 copy-done
  279.8 7.9 %add_rows.1 = (f32[3144,1024]{1,0:T(8,128)S(1)}, f32[3144,1024]{1,0:T(8,128)}, f32[1024,256]{1,0:T(8,128)}, f32[256,1024]{1,0:T(8,128)}) custom-call(s32[3,2048]{1,0:T(4,128)S(1)} %copy-done, bf16[2048,1024]{1,0:T(8,128)(2,1)S(1)} %bitcast.7, f32[3144,1024]{1,0:T(8,128)S(1)} %get-tuple-element.36.de_ref, ...), custom_call_target="tpu_custom_call", output_to_operand_aliasing={{0}: (2, {})} | custom-call | tf_op jit(solution)/shard_map/add_rows/pallas_call | solution.py:973
Async XLA Ops:
  196.1 83.7 %copy-start = (s32[3,2048]{1,0:T(4,128)S(1)}, s32[3,2048]{1,0:T(4,128)}, u32[]{:S(2)}) copy-start(s32[3,2048]{1,0:T(4,128)} %get-tuple-element.27.order) | copy-start | bytes 73732

commit v3 on v2

--- a/solution.py
+++ b/solution.py
@@ -132,6 +132,8 @@
         for pair in pairs:
             s(*pair, j, 2, recv).wait_recv()
             on_block(*pair, j, SIDE - 1)
+        if j % 2:
+            yield
     for a, (buf, start, size) in enumerate(bufs):
         sent = buf.at[pl.ds(0, SIDE * SIDE - 1), pl.ds(start, size)]
         remote(sent, sent, send_sem.at[base + a], recv_sem.at[0], {'tp': plane.at(1, 0)}).wait_send()
@@ -789,12 +791,13 @@
     grad_one[:] = jnp.zeros_like(grad_one)
     grad_two[:] = jnp.zeros_like(grad_two)
 
-    def weights(lo, hi):
+    def weights(ahead):
         step = SIDE
 
-        @pl.loop(lo, hi)
-        def _(c):
-            part = pl.ds(c * step, step)
+        @pl.loop(0, 2)
+        def _(i):
+            row = lax.rem(plane.z + (1 + i if ahead else SIDE - i), SIDE)
+            part = pl.ds(row * step, step)
             x_act = x_all[part].reshape(step * x_all.shape[1], width)
             grad_y = dy_all[part].reshape(step * x_all.shape[1], width)
             hidden = dot(x_act, w_one_buf[:])
@@ -842,20 +845,21 @@
                 if kind == 'x' and 'x' not in order[:i]:
                     pl.when(stage > 0)(spread.arrive)
                 next(steps[kind])
-            drain(steps['d'])
+            next(steps['d'])
             drain(steps['a'] or ())
 
         def onward(rest=rest, steps=steps):
             for kind in rest:
                 next(steps[kind])
+            drain(steps['d'])
 
         pl.when(here)(arrived)
         runs.append((here, onward, functools.partial(drain, steps['x'])))
 
-    weights(0, 2)
+    weights(False)
     for here, onward, _ in runs:
         pl.when(here)(onward)
-    weights(2, SIDE)
+    weights(True)
     for here, _, finish in runs:
         pl.when(here)(finish)
 

time: 290 us -> 287 us (0.990)
  Pallas kernels: 287 us -> 284 us
    pallas_call x1, Pallas kernels: 83.7 us -> 80.7 us  [device_fn(): pl.pallas_call(functools.partial(backward_kernel, last, step), out_shape=...]
where the time goes in v3:
time: 287 us; the launch traced here: 286 us
  Pallas kernels  284 us (99%)
    pallas_call x1, Pallas kernels, device_fn(): pl.pallas_call(functools.partial(forward_kernel, last), out_shape=(many_b...  158 us
    pallas_call x1, Pallas kernels, device_fn(): pl.pallas_call(functools.partial(backward_kernel, last, step), out_shape=...  80.7 us
    pallas_call x1, Pallas kernels, device_fn(): pl.pallas_call(functools.partial(head_kernel, last, pp_size, chunk), out_...  37 us
    pallas_call x1, Pallas kernels, device_fn(): pl.pallas_call(functools.partial(add_kernel, 12), out_shape=(VM((vocab_ro...  7.65 us

profile of v3, /device:TPU:1, one launch (start us, length us, event | category | flops | bytes accessed | tf_op | source)
XLA Modules:
  0.0 286.2 jit_solution(10322578339550568792)
XLA Ops:
  0.6 158.5 %forward_chain.1 = (bf16[16,128,1024]{2,1,0:T(8,128)(2,1)S(1)}, bf16[16,1024]{1,0:T(8,128)(2,1)S(1)}, bf16[3144,1024]{1,0:T(8,128)(2,1)S(1)}, s32[3,2048]{1,0:T(...) custom-call(s32[32,64]{1,0:T(8,128)} %tokens.1, ...), custom_call_target="tpu_custom_call" | custom-call | tf_op jit(solution)/shard_map/forward_chain/pallas_call | solution.py:939
  159.1 37.0 %head.1 = (f32[1,1]{1,0:T(1,128)}, bf16[8,16,1024]{2,1,0:T(8,128)(2,1)}, bf16[3144,2048]{1,0:T(8,128)(2,1)}, bf16[2048,1024]{1,0:T(8,128)(2,1)}) custom-call(bf16[3144,1024]{1,0:T(8,128)(2,1)S(1)} %get-tuple-element.23.table, bf16[16,128,1024]{2,1,0:T(8,128)(2,1)S(1)} %get-tuple-element.24.top, bf16[16,1024]{1,0:T(8,128)(2,1)S(1)} %get-tuple-element.25.own_x, ...), custom_call_target="tpu_custom_call" | custom-call | tf_op jit(solution)/shard_map/head/pallas_call | solution.py:953
  196.1 0.0 copy-start
  196.1 80.7 %backward_chain.1 = (f32[3144,1024]{1,0:T(8,128)S(1)}, bf16[16,128,1024]{2,1,0:T(8,128)(2,1)S(1)}, f32[1024,256]{1,0:T(8,128)S(1)}, f32[256,1024]{1,0:T(8,128)S(1)}) custom-call(bf16[128,1024]{1,0:T(8,128)(2,1)} %bitcast.12, f32[16,128,256]{2,1,0:T(8,128)} %get-tuple-element.29.hid_in, bf16[16,1024,256]{2,1,0:T(8,128)(2,1)} %get-tuple-element.30.two_all, ...), custom_call_target="tpu_custom_call" | custom-call | tf_op jit(solution)/shard_map/backward_chain/pallas_call | solution.py:965
  276.8 0.0 copy-done
  276.8 7.7 %add_rows.1 = (f32[3144,1024]{1,0:T(8,128)S(1)}, f32[3144,1024]{1,0:T(8,128)}, f32[1024,256]{1,0:T(8,128)}, f32[256,1024]{1,0:T(8,128)}) custom-call(s32[3,2048]{1,0:T(4,128)S(1)} %copy-done, bf16[2048,1024]{1,0:T(8,128)(2,1)S(1)} %bitcast.7, f32[3144,1024]{1,0:T(8,128)S(1)} %get-tuple-element.36.de_ref, ...), custom_call_target="tpu_custom_call", output_to_operand_aliasing={{0}: (2, {})} | custom-call | tf_op jit(solution)/shard_map/add_rows/pallas_call | solution.py:977
Async XLA Ops:
  196.1 80.7 %copy-start = (s32[3,2048]{1,0:T(4,128)S(1)}, s32[3,2048]{1,0:T(4,128)}, u32[]{:S(2)}) copy-start(s32[3,2048]{1,0:T(4,128)} %get-tuple-element.27.order) | copy-start | bytes 73732

commit v4 on v3

--- a/solution.py
+++ b/solution.py
@@ -829,7 +829,7 @@
     def _():
         next(a_steps())
 
-    planes = [(stage <= 1, None, 'dxddxdxdxdx', 'xx'), ((stage > 1) & lower, None, 'dddxdxdxdx', 'xxx'),
+    planes = [(stage <= 1, None, 'xddxdxdxdxdx', 'x'), ((stage > 1) & lower, None, 'dddxdxdxdx', 'xxx'),
               (mid, mid_steps, 'dtdadatdaxdaxdx', 'xxx'), (upper & jnp.logical_not(mid), a_steps(True), 'datdadatdaxdaxdax', 'xxx')]
     runs = []
     for here, more, order, rest in planes:
@@ -869,8 +869,9 @@
     pl.when(stage == 1)(hop.wait_send)
 
 
-def add_kernel(pieces, order, dx_ref, de_ref, one_ref, two_ref, de_out, table_out, one_out, two_out, wide, sem):
-    saves = [local(one_ref, one_out, sem.at[0]), local(two_ref, two_out, sem.at[1])]
+def add_kernel(pieces, order, dx_ref, de_ref, loss_ref, one_ref, two_ref, de_out, loss_out, table_out, one_out, two_out, wide, sem):
+    small = ((one_ref, one_out), (two_ref, two_out), (loss_ref, loss_out))
+    saves = [local(*pair, sem.at[i]) for i, pair in enumerate(small)]
     for save in saves:
         save.start()
     wide[:] = dx_ref[:].astype(F32)
@@ -884,7 +885,7 @@
     size = -(-rows // (8 * pieces)) * 8
     for c in range(pieces):
         part = pl.ds(c * size, min(size, rows - c * size))
-        saves.append(local(de_out.at[part], table_out.at[part], sem.at[2 + c]))
+        saves.append(local(de_out.at[part], table_out.at[part], sem.at[len(small) + c]))
         saves[-1].start()
     for save in saves:
         save.wait()
@@ -952,7 +953,7 @@
         by_pair = (num_tokens // pair, pair // group, group)
         loss, g_top, g_all, n_all = pl.pallas_call(
             functools.partial(head_kernel, last, pp_size, chunk),
-            out_shape=(shape((1, 1), F32), pltpu.HBM((pp_size, unit, width), BF16), shape((vocab_rows, num_tokens), BF16), shape((num_tokens, width), BF16)),
+            out_shape=(VM((1, 1), F32), pltpu.HBM((pp_size, unit, width), BF16), shape((vocab_rows, num_tokens), BF16), shape((num_tokens, width), BF16)),
             in_specs=[vmem()] * 4,
             out_specs=[vmem()] * 2 + [anywhere()] * 2,
             scratch_shapes=[VM((num_tokens, width), BF16), VM((pp_size, group), jnp.int32), VM((3, vocab_rows, group), BF16),
@@ -974,13 +975,13 @@
         )(g_top.reshape(block, width), hidden, two_t, one_t, g_all, n_all, x_all, w_one, w_two)
 
         smem = pl.BlockSpec(memory_space=pltpu.SMEM)
-        _, grad_table, grad_one, grad_two = pl.pallas_call(
+        _, loss, grad_table, grad_one, grad_two = pl.pallas_call(
             functools.partial(add_kernel, 12),
-            out_shape=(VM((vocab_rows, width), F32), shape((vocab_rows, width), F32), shape((width, cols), F32), shape((cols, width), F32)),
-            in_specs=[smem] + [vmem()] * 4, out_specs=[vmem()] + [anywhere()] * 3,
-            scratch_shapes=[VM((num_tokens, width), F32), DMA((14,))], input_output_aliases={2: 0},
+            out_shape=(VM((vocab_rows, width), F32), shape((1, 1), F32), shape((vocab_rows, width), F32), shape((width, cols), F32), shape((cols, width), F32)),
+            in_specs=[smem] + [vmem()] * 5, out_specs=[vmem()] + [anywhere()] * 4,
+            scratch_shapes=[VM((num_tokens, width), F32), DMA((15,))], input_output_aliases={2: 0},
             compiler_params=pltpu.CompilerParams(vmem_limit_bytes=24 << 20), name='add_rows',
-        )(order, dx_first.reshape(num_tokens, width), de_head, grad_one, grad_two)
+        )(order, dx_first.reshape(num_tokens, width), de_head, loss, grad_one, grad_two)
         return loss.reshape(1), grad_one[None], grad_two[None], grad_table
 
     return jax.shard_map(device_fn, mesh=mesh, in_specs=(P('dp', None), P('dp', None), P('tp', None), P('pp', None, 'tp'), P('pp', 'tp', None)), out_specs=(P('dp'), P(('dp', 'pp'), None, 'tp'), P(('dp', 'pp'), 'tp', None), P(('dp', 'tp'), None)), check_vma=False)

time: 287 us -> 285 us (level)
  no operation moved by 1% of the time
where the time goes in v4:
time: 285 us
  Pallas kernels  284 us (100%)
    pallas_call x1, Pallas kernels, device_fn(): pl.pallas_call(functools.partial(forward_kernel, last), out_shape=(many_b...  158 us
    pallas_call x1, Pallas kernels, device_fn(): pl.pallas_call(functools.partial(backward_kernel, last, step), out_shape=...  80 us
    pallas_call x1, Pallas kernels, device_fn(): pl.pallas_call(functools.partial(head_kernel, last, pp_size, chunk), out_...  37 us
    pallas_call x1, Pallas kernels, device_fn(): pl.pallas_call(functools.partial(add_kernel, 12), out_shape=(VM((vocab_ro...  8.45 us

profile of v4, /device:TPU:1, one launch (start us, length us, event | category | flops | bytes accessed | tf_op | source)
XLA Modules:
  0.0 284.8 jit_solution(14257202389666055787)
XLA Ops:
  0.6 158.5 %forward_chain.1 = (bf16[16,128,1024]{2,1,0:T(8,128)(2,1)S(1)}, bf16[16,1024]{1,0:T(8,128)(2,1)S(1)}, bf16[3144,1024]{1,0:T(8,128)(2,1)S(1)}, s32[3,2048]{1,0:T(...) custom-call(s32[32,64]{1,0:T(8,128)} %tokens.1, ...), custom_call_target="tpu_custom_call" | custom-call | tf_op jit(solution)/shard_map/forward_chain/pallas_call | solution.py:940
  159.1 37.0 %head.1 = (f32[1,1]{1,0:T(1,128)}, bf16[8,16,1024]{2,1,0:T(8,128)(2,1)}, bf16[3144,2048]{1,0:T(8,128)(2,1)}, bf16[2048,1024]{1,0:T(8,128)(2,1)}) custom-call(bf16[3144,1024]{1,0:T(8,128)(2,1)S(1)} %get-tuple-element.25.table, bf16[16,128,1024]{2,1,0:T(8,128)(2,1)S(1)} %get-tuple-element.26.top, bf16[16,1024]{1,0:T(8,128)(2,1)S(1)} %get-tuple-element.27.own_x, ...), custom_call_target="tpu_custom_call" | custom-call | tf_op jit(solution)/shard_map/head/pallas_call | solution.py:954
  196.1 0.0 copy-start
  196.1 80.0 %backward_chain.1 = (f32[3144,1024]{1,0:T(8,128)S(1)}, bf16[16,128,1024]{2,1,0:T(8,128)(2,1)S(1)}, f32[1024,256]{1,0:T(8,128)S(1)}, f32[256,1024]{1,0:T(8,128)S(1)}) custom-call(bf16[128,1024]{1,0:T(8,128)(2,1)} %bitcast.12, f32[16,128,256]{2,1,0:T(8,128)} %get-tuple-element.29.hid_in, bf16[16,1024,256]{2,1,0:T(8,128)(2,1)} %get-tuple-element.30.two_all, ...), custom_call_target="tpu_custom_call" | custom-call | tf_op jit(solution)/shard_map/backward_chain/pallas_call | solution.py:966
  276.1 0.0 copy-done
  276.1 8.5 %add_rows.1 = (f32[3144,1024]{1,0:T(8,128)S(1)}, f32[1,1]{1,0:T(1,128)}, f32[3144,1024]{1,0:T(8,128)}, f32[1024,256]{1,0:T(8,128)}, f32[256,1024]{1,0:T(8,128)}) custom-call(s32[3,2048]{1,0:T(4,128)S(1)} %copy-done, bf16[2048,1024]{1,0:T(8,128)(2,1)S(1)} %bitcast.7, f32[3144,1024]{1,0:T(8,128)S(1)} %get-tuple-element.36.de_ref, ...), custom_call_target="tpu_custom_call", output_to_operand_aliasing={{0}: (2, {})} | custom-call | tf_op jit(solution)/shard_map/add_rows/pallas_call | solution.py:978
Async XLA Ops:
  196.1 80.0 %copy-start = (s32[3,2048]{1,0:T(4,128)S(1)}, s32[3,2048]{1,0:T(4,128)}, u32[]{:S(2)}) copy-start(s32[3,2048]{1,0:T(4,128)} %get-tuple-element.24.order) | copy-start | bytes 73732

commit v5 on v4

--- a/solution.py
+++ b/solution.py
@@ -327,7 +327,6 @@
     moves = ((emb, table), (w_one, ones.at[tp]), (w_two, twos.at[tp]), (one_t, one_out), (two_t, two_out), (hid_ref, hid_out), (x_all, x_out))
     load, own_one, own_two, *saves = [local(src, dst, loc_sem.at[i]) for i, (src, dst) in enumerate(moves)]
     save_one, save_two, save_hid, save_x = saves
-    load.start()
     own_one.start()
     own_two.start()
     for peer in plane.rings() + [{'pp': lax.rem(stage + d, stages)} for d in range(1, stages)]:
@@ -335,6 +334,7 @@
 
     own_one.wait()
     own_two.wait()
+    load.start()
     pl.semaphore_wait(pltpu.get_barrier_semaphore(), 6 + last)
     def weight_steps(begun=False):
         return plane_gather(plane, [(ones, 0, ones.shape[1]), (twos, 0, twos.shape[1])], send_sem, recv_sem, begun=begun)

time: 285 us -> 285 us (level)
  no operation moved by 1% of the time
where the time goes in v5:
time: 285 us
  Pallas kernels  284 us (100%)
    pallas_call x1, Pallas kernels, device_fn(): pl.pallas_call(functools.partial(forward_kernel, last), out_shape=(many_b...  158 us
    pallas_call x1, Pallas kernels, device_fn(): pl.pallas_call(functools.partial(backward_kernel, last, step), out_shape=...  80 us
    pallas_call x1, Pallas kernels, device_fn(): pl.pallas_call(functools.partial(head_kernel, last, pp_size, chunk), out_...  37 us
    pallas_call x1, Pallas kernels, device_fn(): pl.pallas_call(functools.partial(add_kernel, 12), out_shape=(VM((vocab_ro...  8.57 us

profile of v5, /device:TPU:1, one launch (start us, length us, event | category | flops | bytes accessed | tf_op | source)
XLA Modules:
  0.0 284.9 jit_solution(11173918507402809235)
XLA Ops:
  0.6 158.5 %forward_chain.1 = (bf16[16,128,1024]{2,1,0:T(8,128)(2,1)S(1)}, bf16[16,1024]{1,0:T(8,128)(2,1)S(1)}, bf16[3144,1024]{1,0:T(8,128)(2,1)S(1)}, s32[3,2048]{1,0:T(...) custom-call(s32[32,64]{1,0:T(8,128)} %tokens.1, ...), custom_call_target="tpu_custom_call" | custom-call | tf_op jit(solution)/shard_map/forward_chain/pallas_call | solution.py:940
  159.1 37.0 %head.1 = (f32[1,1]{1,0:T(1,128)}, bf16[8,16,1024]{2,1,0:T(8,128)(2,1)}, bf16[3144,2048]{1,0:T(8,128)(2,1)}, bf16[2048,1024]{1,0:T(8,128)(2,1)}) custom-call(bf16[3144,1024]{1,0:T(8,128)(2,1)S(1)} %get-tuple-element.25.table, bf16[16,128,1024]{2,1,0:T(8,128)(2,1)S(1)} %get-tuple-element.26.top, bf16[16,1024]{1,0:T(8,128)(2,1)S(1)} %get-tuple-element.27.own_x, ...), custom_call_target="tpu_custom_call" | custom-call | tf_op jit(solution)/shard_map/head/pallas_call | solution.py:954
  196.1 0.0 copy-start
  196.1 80.0 %backward_chain.1 = (f32[3144,1024]{1,0:T(8,128)S(1)}, bf16[16,128,1024]{2,1,0:T(8,128)(2,1)S(1)}, f32[1024,256]{1,0:T(8,128)S(1)}, f32[256,1024]{1,0:T(8,128)S(1)}) custom-call(bf16[128,1024]{1,0:T(8,128)(2,1)} %bitcast.12, f32[16,128,256]{2,1,0:T(8,128)} %get-tuple-element.29.hid_in, bf16[16,1024,256]{2,1,0:T(8,128)(2,1)} %get-tuple-element.30.two_all, ...), custom_call_target="tpu_custom_call" | custom-call | tf_op jit(solution)/shard_map/backward_chain/pallas_call | solution.py:966
  276.1 0.0 copy-done
  276.1 8.6 %add_rows.1 = (f32[3144,1024]{1,0:T(8,128)S(1)}, f32[1,1]{1,0:T(1,128)}, f32[3144,1024]{1,0:T(8,128)}, f32[1024,256]{1,0:T(8,128)}, f32[256,1024]{1,0:T(8,128)}) custom-call(s32[3,2048]{1,0:T(4,128)S(1)} %copy-done, bf16[2048,1024]{1,0:T(8,128)(2,1)S(1)} %bitcast.7, f32[3144,1024]{1,0:T(8,128)S(1)} %get-tuple-element.36.de_ref, ...), custom_call_target="tpu_custom_call", output_to_operand_aliasing={{0}: (2, {})} | custom-call | tf_op jit(solution)/shard_map/add_rows/pallas_call | solution.py:978
Async XLA Ops:
  196.1 80.0 %copy-start = (s32[3,2048]{1,0:T(4,128)S(1)}, s32[3,2048]{1,0:T(4,128)}, u32[]{:S(2)}) copy-start(s32[3,2048]{1,0:T(4,128)} %get-tuple-element.24.order) | copy-start | bytes 73732
